TPU v7x, 32 devices: a whole 2x2x4 slice. The times are simulated.
32 devices in a mesh: tp: 4 (over z), pp: 8 (over y, x, core).
Axes of the slice: x: 2, y: 2, z: 4, core: 2. Of those that a mesh axis runs over, the one named last changes fastest.
Arguments:
- tokens: bfloat16 [8192, 8192], P('pp', 'tp'), may hold values from -60 to 60
- norm_gain: bfloat16 [8192], P('tp'), may hold values from 0.099609375 to 1.8984375
- weights_gen: bfloat16 [8, 1280, 8192], P('tp', None, 'pp'), may hold values from -2 to 2
- segment_ids: int32 [8, 1024], P('pp'), may hold values from 0 to 15, never falling along the last dimension, each value on 1 to 512 neighbouring positions
Outputs:
- weights_rows: bfloat16 [8, 1280, 8192], P('tp', 'pp')
- attended: bfloat16 [8192, 8192], P('pp', 'tp')
Inputs may be any that keep to these rules, and one draw needn't show every extreme that they name: `segment_ids`: ids never fall along a block; every sequence has 1 to 512 tokens and lies in one block.
All inputs are finite; a program needn't handle non-finite values.
Results may differ from a plain program's by a relative error of at most 0.0075.
Values may be sent and summed in bfloat16 or wider, within the bound.
No kernel may reach another device: no remote copies, remote signals or barrier semaphores. Data moves between devices by JAX's collectives and lax.ppermute only.
A program may use at most 192 MiB of HBM per device.

v0:
```python
import math

import jax
import jax.numpy as jnp
from jax import lax
from jax.sharding import PartitionSpec as P

DH = 128
GROUP = 8


rope_base = 500000.0


def rotary(values, positions):
    half = values.shape[-1] // 2
    freq = jnp.exp(
        jnp.arange(half, dtype=jnp.float32) * (-2.0 * math.log(rope_base) / values.shape[-1])
    )
    angle = positions.astype(jnp.float32)[:, None] * freq[None, :]
    cosine = jnp.cos(angle)
    sine = jnp.sin(angle)
    extra = values.ndim - 2
    cosine = cosine.reshape(cosine.shape[:1] + (1,) * extra + cosine.shape[1:])
    sine = sine.reshape(sine.shape[:1] + (1,) * extra + sine.shape[1:])
    first = values[..., :half]
    second = values[..., half:]
    return jnp.concatenate(
        [first * cosine - second * sine, second * cosine + first * sine], axis=-1
    )


def shards(tokens, norm_gain, weights_gen, segment_ids):
    weights_rows = lax.all_to_all(weights_gen, "pp", split_axis=1, concat_axis=2, tiled=True)
    gathered, gain = (
        lax.all_gather(tokens, "tp", axis=1, tiled=True),
        lax.all_gather(norm_gain, "tp", axis=0, tiled=True),
    )
    floats = gathered.astype(jnp.float32)
    square = jnp.mean(floats * floats, axis=-1, keepdims=True)
    normed = (floats * lax.rsqrt(square + 1e-05) * gain.astype(jnp.float32)).astype(jnp.bfloat16)
    count = normed.shape[0]
    groups = weights_gen.shape[0]
    mixed = jnp.einsum(
        "td,grd->tgr",
        normed,
        lax.all_gather(weights_rows, "pp", axis=1, tiled=True),
        preferred_element_type=jnp.float32,
    )
    mixed = mixed.reshape(count, groups, GROUP + 2, DH)
    seg = segment_ids[0]
    order = jnp.arange(count, dtype=jnp.int32)
    start_index = jnp.sum((seg[None, :] < seg[:, None]).astype(jnp.int32), axis=1)
    positions = order - start_index
    query = rotary(mixed[:, :, :GROUP, :], positions).astype(jnp.bfloat16)
    key_heads = rotary(mixed[:, :, GROUP, :], positions).astype(jnp.bfloat16)
    value_heads = mixed[:, :, GROUP + 1, :].astype(jnp.bfloat16)
    score = jnp.einsum("tgjd,sgd->gjts", query, key_heads, preferred_element_type=jnp.float32) * (
        1.0 / math.sqrt(DH)
    )
    allowed = (seg[:, None] == seg[None, :]) & (order[:, None] >= order[None, :])
    score = jnp.where(allowed[None, None], score, -1e30)
    top = jnp.max(score, axis=-1, keepdims=True)
    expo = jnp.where(allowed[None, None], jnp.exp(score - top), 0.0)
    prob = (expo / jnp.sum(expo, axis=-1, keepdims=True)).astype(jnp.bfloat16)
    output = jnp.einsum("gjts,sgd->tgjd", prob, value_heads, preferred_element_type=jnp.float32)
    attended = output.astype(jnp.bfloat16).reshape(count, groups * GROUP * DH)
    return (weights_rows, attended)


def solution(mesh):
    in_specs = (P("pp", "tp"), P("tp"), P("tp", None, "pp"), P("pp", None))
    out_specs = (P("tp", "pp", None), P("pp", "tp"))
    return jax.shard_map(shards, mesh=mesh, in_specs=in_specs, out_specs=out_specs, check_vma=False)
```

profile of v0, /device:TPU:0, one launch (start us, length us, event | category | flops | bytes accessed | tf_op | source)
XLA Modules:
  0.0 658.1 jit_solution(8889944450149644430)
XLA Ops:
  7.2 0.7 all-gather.3.cloned.1.call-update
  7.9 0.0 all-gather.5.cloned.1.call-start
  7.9 9.4 %copy.21 = bf16[2,1280,1024]{2,0,1:T(2,128)(2,1)S(1)} copy(bf16[2,1280,1024]{2,1,0:T(8,128)(2,1)} %param.6) | data formatting | bytes 10485760 | tf_op args[2]
  17.4 65.3 %all_to_all.18 = bf16[2,1280,1024]{2,0,1:T(2,128)(2,1)S(1)} all-to-all(bf16[2,1280,1024]{2,0,1:T(2,128)(2,1)S(1)} %copy.21), channel_id=1, replica_groups=mesh['tp'=4,'pp'=8] {'pp'}, dimensions={1} | all-to-all | bytes 10485760 | tf_op jit(solution)/shard_map/all_to_all | solution.py:34
  82.6 5.2 copy.43
  87.8 8.9 %all_to_all.16 = bf16[2,160,8192]{2,1,0:T(8,128)(2,1)} reshape(bf16[2,160,8,1024]{3,2,1,0:T(8,128)(2,1)} %bitcast.49) | data formatting | bytes 10485760 | tf_op jit(solution)/shard_map/all_to_all | solution.py:34
  96.8 24.4 %all_gather.10 = bf16[8192]{0:T(1024)(128)(2,1)S(1)} all-gather(bf16[2048]{0:T(1024)(128)(2,1)S(1)} %copy-done.2), channel_id=1, replica_groups=mesh['tp'=4,'pp'=8] {'tp'}, dimensions={0}, use_global_device_ids=true | all-gather | bytes 20480 | tf_op jit(solution)/shard_map/all_gather | solution.py:37
  121.2 0.5 convert_reduce_fusion
  121.7 1.9 multiply_cosine_fusion
  123.6 1.6 fusion.16
  125.1 174.1 %all-gather.3.cloned.1.call-done = bf16[1024,8192]{1,0:T(8,128)(2,1)} async-done(((bf16[1024,2048]{1,0:T(8,128)(2,1)}), bf16[1024,8192]{1,0:T(8,128)(2,1)}) %all-gather.3.cloned.1.call-update) | async-done | bytes 16777232 | tf_op jit(solution)/shard_map/all_gather | solution.py:36
  299.3 7.2 %fusion.2 = f32[1024]{0:T(1024)S(1)} fusion(bf16[1024,8192]{1,0:T(8,128)(2,1)} %all-gather.3.cloned.1.call-done), kind=kLoop, calls=%fused_computation.7 | loop fusion | flops 25164800 | bytes 16781312 | tf_op jit(solution)/shard_map/reduce_sum | solution.py:40
  306.5 189.8 %all-gather.5.cloned.1.call-done = bf16[2,1280,8192]{2,1,0:T(8,128)(2,1)} async-done(((bf16[2,160,8192]{2,1,0:T(8,128)(2,1)}), bf16[2,1280,8192]{2,1,0:T(8,128)(2,1)}) %all-gather.5.cloned.1.call-update) | async-done | bytes 41943056 | tf_op jit(solution)/shard_map/all_gather | solution.py:47
  496.3 54.2 %fusion.10 = f32[1024,2,1280]{0,2,1:T(8,128)} fusion(bf16[2,1280,8192]{2,1,0:T(8,128)(2,1)} %all-gather.5.cloned.1.call-done, bf16[1024,8192]{1,0:T(8,128)(2,1)} %all-gather.3.cloned.1.call-done, f32[8192]{0:T(1024)S(1)} %convert_element_type.36, f32[1024]{0:T(1024)S(1)} %add_rsqrt_fusion), kind=kOutput, calls=%fused_computation.15 | convolution fusion | flops 42983227392 | bytes 69242880 | tf_op jit(solution)/shard_map/td,grd->tgr/dot_general | solution.py:44
  550.5 1.3 slice.29
  551.8 8.5 %fusion.27 = (f32[1024,2,8,64]{0,3,2,1:T(8,128)}, f32[1024,2,8,64]{0,3,2,1:T(8,128)}) fusion(f32[1024,2,10,128]{0,3,2,1:T(8,128)} %bitcast.52), kind=kLoop, calls=%fused_computation.42 | loop fusion | bytes 16777216 | tf_op jit(solution)/shard_map/slice | solution.py:27
  560.2 0.3 copy.34
  560.5 6.9 %copy.36 = f32[1024,2,8,64]{3,0,2,1:T(8,128)} copy(f32[1024,2,8,64]{0,3,2,1:T(8,128)} %get-tuple-element.10) | data formatting | bytes 8388608
  567.5 6.9 %copy.35 = f32[1024,2,8,64]{3,0,2,1:T(8,128)} copy(f32[1024,2,8,64]{0,3,2,1:T(8,128)} %get-tuple-element.11) | data formatting | bytes 8388608
  574.3 0.4 subtract_convert_fusion.1
  574.8 9.6 %subtract_convert_fusion = (bf16[1024,2,8,64]{3,0,2,1:T(8,128)(2,1)}, bf16[1024,2,8,64]{3,0,2,1:T(8,128)(2,1)}) fusion(f32[1024,2,8,64]{3,0,2,1:T(8,128)} %copy.36, f32[1024,2,8,64]{3,0,2,1:T(8,128)} %copy.35, f32[1024,64]{1,0:T(8,128)S(1)} %get-tuple-element.15, f32[1024,64]{1,0:T(8,128)S(1)} %get-tuple-element.14), kind=kLoop, calls=%fused_computation.19 | loop fusion | flops 8388608 | bytes 13107200 | tf_op jit(solution)/shard_map/convert
  584.4 36.3 %fusion.28 = (f32[2,8,1024]{2,1,0:T(8,128)S(1)}, f32[2,8,1024,1024]{2,3,1,0:T(8,128)}) fusion(pred[1024,1024]{0,1:T(8,128)(4,1)S(1)} %copy-done, bf16[1024,2,8,64]{3,0,2,1:T(8,128)(2,1)} %get-tuple-element.9, bf16[1024,2,8,64]{3,0,2,1:T(8,128)(2,1)} %get-tuple-element.8, bf16[1024,2,64]{2,0,1:T(8,128)(2,1)S(1)} %get-tuple-element.13, ...), kind=kOutput, calls=%fused_computation.43 | convolution fusion | flops 4388291584 | bytes 72941568 | tf_op jit(solution)/shard_map/sub | solution.py:64
  620.7 24.1 %fusion.17 = bf16[2,128,8,1024]{3,1,2,0:T(8,128)(2,1)} fusion(f32[2,8,1024,1024]{2,3,1,0:T(8,128)} %get-tuple-element.17, f32[2,8,1024]{2,1,0:T(8,128)S(1)} %get-tuple-element.16, f32[1024,2,10,128]{0,3,2,1:T(8,128)} %bitcast.53), kind=kOutput, calls=%fused_computation.26 | convolution fusion | flops 4330618880 | bytes 71892992 | tf_op jit(solution)/shard_map/gjts,sgd->tgjd/dot_general | solution.py:66
  644.8 6.4 copy.29
  (12 shorter events, 0.1 us)
Async XLA Ops:
  7.2 292.1 %all-gather.3.cloned.1.call-start = ((), (), s32[]{:S(2)}) async-start(), calls=%async_computation.1 | async-start | bytes 20971520 | tf_op jit(solution)/shard_map/all_gather | solution.py:36
  7.9 488.4 %all-gather.5.cloned.1.call-start = ((), (), s32[]{:S(2)}) async-start(), calls=%async_computation.2 | async-start | bytes 47185920 | tf_op jit(solution)/shard_map/all_gather | solution.py:47
  87.8 8.9 %copy-start.2 = (bf16[2048]{0:T(1024)(128)(2,1)S(1)}, bf16[2048]{0:T(1024)(128)(2,1)}, u32[]{:S(2)}) copy-start(bf16[2048]{0:T(1024)(128)(2,1)} %param.5) | copy-start | bytes 12292
  87.8 33.3 %copy-start.1 = (s32[1,1024]{1,0:T(1,128)S(1)}, s32[1,1024]{1,0:T(1,128)}, u32[]{:S(2)}) copy-start(s32[1,1024]{1,0:T(1,128)} %param.7) | copy-start | bytes 12292
  574.7 9.7 %copy-start = (pred[1024,1024]{0,1:T(8,128)(4,1)S(1)}, pred[1024,1024]{0,1:T(8,128)(4,1)}, u32[]{:S(2)}) copy-start(pred[1024,1024]{0,1:T(8,128)(4,1)} %fusion.16) | copy-start | bytes 3145732
Sparse Core Ops, SparseCore 0:
  9.5 289.6 all-gather.2
  301.7 194.4 all-gather.4
where the time goes:
time: 659 us; the launch traced here: 658 us
  waiting for transfers between devices  365 us (55%)
  matrix products  115 us (17%)
  blocking collectives  89.6 us (14%)
  local copies, waits for them, and re-layouts  53.8 us (8%)
  other arithmetic  21.2 us (3%)
  between operations  14.1 us (2%)
    all_gather x1, waiting for transfers between devices, shards(): lax.all_gather(weights_rows, 'pp', axis=1, tiled=True)  190 us
    all_gather x1, waiting for transfers between devices, shards(): lax.all_gather(tokens, 'tp', axis=1, tiled=True)  174 us
    all_to_all x1, blocking collectives, shards(): lax.all_to_all(weights_gen, 'pp', split_axis=1, concat_axis=2, tiled=True)  65.3 us
    dot_general x1, matrix products, shards(): jnp.einsum('td,grd->tgr', normed, lax.all_gather(weights_rows, 'pp', axis...  54.2 us
    sub x1, matrix products, shards(): expo = jnp.where(allowed[None, None], jnp.exp(score - top), 0.0)  36.3 us
    unnamed x11, local copies, waits for them, and re-layouts  29.9 us
    all_gather x1, blocking collectives, shards(): lax.all_gather(norm_gain, 'tp', axis=0, tiled=True)  24.4 us
    dot_general x1, matrix products, shards(): jnp.einsum('gjts,sgd->tgjd', prob, value_heads, preferred_element_type=jn...  24.1 us
  transfers between devices with their start and end apart: 2, of which 2 were waited for; matrix products, arithmetic and copies ran while one was open for 4% of the time, Pallas kernels for 0%

commit v1 on v0

v1 whole, which is shorter than its diff:
```python
import functools
import math

import jax
import jax.numpy as jnp
from jax import lax
from jax.experimental import pallas as pl
from jax.experimental.pallas import tpu as pltpu
from jax.sharding import PartitionSpec as P


DH = 128
GROUP = 8
SPAN = 512
PAIR = 2 * DH
CHUNKS = 4
BF16 = jnp.bfloat16
F32 = jnp.float32

rope_base = 500000.0


NT = (((1,), (1,)), ((), ()))
NN = (((1,), (0,)), ((), ()))


def dot(a, b, dims):
    return lax.dot_general(a, b, dims, preferred_element_type=F32)


def params(mib=56):
    return pltpu.CompilerParams(vmem_limit_bytes=mib << 20)


def any_spec():
    return pl.BlockSpec(memory_space=pl.ANY)


def normalise(x_ref, inv_ref, gain, rows, start, put):
    step = min(rows, 16)

    @pl.loop(0, rows // step, unroll=4)
    def _(i):
        r = pl.multiple_of(i * step, step)
        x = x_ref[pl.ds(r, step), :].astype(F32)
        y = x * inv_ref[pl.ds(start + r, step), :] * gain
        put(start + r, step, y.astype(BF16))


def place_kernel(pieces, old, groups, slices, where_ref, *refs):
    count = len(pieces)
    ins = refs[:count]
    out, rows_out, buf, sem_in, sem_out, sem_rows = refs[count + 2 * old :]
    width = out.shape[2]
    own = out.shape[1] // groups // slices
    me = where_ref[0]
    spots = []
    used = 0
    for which, first, size in pieces:
        spots.append(pl.ds(used, size))
        used += size

    def get(i):
        return pltpu.make_async_copy(ins[i], buf.at[spots[i]], sem_in.at[i])

    def put(i):
        which, first, size = pieces[i]
        at = out.at[where_ref[1 + which], pl.ds(first, size), :]
        return pltpu.make_async_copy(buf.at[spots[i]], at, sem_out.at[i])

    def each(i, act):
        which, first, size = pieces[i]
        col = pl.multiple_of(where_ref[1 + which] * width, width)
        for g in range(groups):
            low, high = g * own * slices, (g + 1) * own * slices
            if high <= first or low >= first + size:
                continue
            at = low + me * own - first

            def go(at=at, col=col, g=g):
                src = buf.at[pl.ds(pl.multiple_of(spots[i].start + at, own), own), :]
                act(pltpu.make_async_copy(src, rows_out.at[g, :, pl.ds(col, width)], sem_rows.at[i, g]))

            if first <= low and high <= first + size:
                go()
            else:
                pl.when((at >= 0) & (at < size))(go)

    for i in range(count):
        get(i).start()
    for i in range(count):
        get(i).wait()
        put(i).start()
        each(i, lambda copy: copy.start())
    for i in range(count):
        put(i).wait()
        each(i, lambda copy: copy.wait())


def place(state, where, items, rows, groups, slices):
    arrays = [x for _, _, x in items]
    pieces = [(which, first, x.shape[0]) for which, first, x in items]
    width = arrays[0].shape[1]
    count = len(arrays)
    total = sum(size for _, _, size in pieces)
    old = 0 if state is None else 1
    grid = pltpu.PrefetchScalarGridSpec(
        num_scalar_prefetch=1,
        grid=(1,),
        in_specs=[any_spec()] * (count + 2 * old),
        out_specs=[any_spec()] * 2,
        scratch_shapes=[
            pltpu.VMEM((total, width), BF16),
            pltpu.SemaphoreType.DMA((count,)),
            pltpu.SemaphoreType.DMA((count,)),
            pltpu.SemaphoreType.DMA((count, groups)),
        ],
    )
    size = total * width * 2
    return pl.pallas_call(
        functools.partial(place_kernel, pieces, old, groups, slices),
        grid_spec=grid,
        out_shape=(
            jax.ShapeDtypeStruct((slices, rows, width), BF16),
            jax.ShapeDtypeStruct((groups, rows // groups // slices, slices * width), BF16),
        ),
        input_output_aliases={count + 1: 0, count + 2: 1} if old else {},
        compiler_params=params(),
        cost_estimate=pl.CostEstimate(flops=size * 100, bytes_accessed=2 * size, transcendentals=0),
        name="place",
    )(where, *arrays, *(state if old else ()))


def prep_kernel(k, x_ref, inv_ref, gain_ref, *refs):
    o_ref = refs[-1]

    def put(r, n, y):
        o_ref[0, pl.ds(r, n), :] = y

    normalise(x_ref, inv_ref, gain_ref[k : k + 1, :], x_ref.shape[0], 0, put)


def prep(k, start, x, inv, gains, out):
    rows, width = x.shape
    block = min(rows, 256)
    at = start // block
    extra = 0 if out is None else 1
    return pl.pallas_call(
        functools.partial(prep_kernel, k),
        grid=(rows // block,),
        in_specs=[
            pl.BlockSpec((block, width), lambda i: (i, 0)),
            pl.BlockSpec((block, 1), lambda i: (at + i, 0)),
            pl.BlockSpec(gains.shape, lambda i: (0, 0)),
        ]
        + [any_spec()] * extra,
        out_specs=pl.BlockSpec((1, block, width), lambda i: (k, at + i, 0)),
        out_shape=jax.ShapeDtypeStruct((gains.shape[0] - 1, inv.shape[0], width), BF16),
        input_output_aliases={3: 0} if extra else {},
        compiler_params=params(),
        cost_estimate=pl.CostEstimate(flops=rows * width * 100, bytes_accessed=rows * width * 4, transcendentals=0),
        name="prep",
    )(x, inv, gains, *([out] if extra else []))


def early_kernel(units, per, old, which_ref, x_hbm, *refs):
    weights = refs[:units]
    acc_ref, xs, sems = refs[-3:]
    _, count, width = xs.shape
    f2 = width // per
    block = min(count, 512)
    first = pl.program_id(0) == 0

    def get(u, i):
        at = pl.ds(pl.multiple_of(i * block, block), block)
        return pltpu.make_async_copy(x_hbm.at[which_ref[u], at], xs.at[u, at], sems.at[u, i])

    @pl.when(first)
    def _():
        for i in range(count // block):
            for u in range(units):
                get(u, i).start()

    @pl.loop(0, count // block)
    def _(i):
        r = pl.ds(pl.multiple_of(i * block, block), block)

        @pl.when(first)
        def _():
            for u in range(units):
                get(u, i).wait()

        if old:
            acc_ref[:, r] = refs[units][:, r]
        else:
            acc_ref[:, r] = jnp.zeros((acc_ref.shape[0], block), F32)
        for u in range(units):

            @pl.when(which_ref[2 * units + u] != 0)
            def _():
                total = acc_ref[:, r]
                for j in range(per):
                    total = total + dot(weights[u][0, j], xs[u, r, j * f2 : (j + 1) * f2], NT)
                acc_ref[:, r] = total


def early(units, which, xs, whole, per, acc):
    _, count, width = xs.shape
    rows = whole.shape[1]
    w4 = whole.reshape(-1, per, rows, whole.shape[2])
    block = 2 * PAIR if rows % (2 * PAIR) == 0 else PAIR
    old = 0 if acc is None else 1

    def wspec(u):
        return pl.BlockSpec((1, per, block, whole.shape[2]), lambda n, f: (f[units + u], 0, n, 0))

    aspec = pl.BlockSpec((block, count), lambda n, f: (n, 0))
    grid = pltpu.PrefetchScalarGridSpec(
        num_scalar_prefetch=1,
        grid=(rows // block,),
        in_specs=[any_spec()] + [wspec(u) for u in range(units)] + [aspec] * old,
        out_specs=aspec,
        scratch_shapes=[
            pltpu.VMEM((units, count, width), BF16),
            pltpu.SemaphoreType.DMA((units, count // min(count, 512))),
        ],
    )
    return pl.pallas_call(
        functools.partial(early_kernel, units, per, old),
        grid_spec=grid,
        out_shape=jax.ShapeDtypeStruct((rows, count), F32),
        input_output_aliases={2 + units: 0} if old else {},
        compiler_params=params(60),
        cost_estimate=pl.CostEstimate(
            flops=2 * count * width * units * rows,
            bytes_accessed=units * width * (rows + count) * 2 + count * rows * 4 * (1 + old),
            transcendentals=0,
        ),
        name="early",
    )(which, xs, *([w4] * units), *([acc] if old else []))


def late_kernel(start, sizes, per, groups, aliased, which_ref, inv_ref, gain_ref, cos_ref, sin_ref, begin_ref, *refs):
    hist = len(sizes)
    keys = refs[:hist]
    values = refs[hist : 2 * hist]
    x_hbm, w_hbm, acc_hbm = refs[2 * hist : 2 * hist + 3]
    out_ref, k_ref, v_ref, x_ref, w_ref, acc_ref, xn, bias, sems = refs[2 * hist + 3 + aliased :]
    rows, width = x_ref.shape
    f2 = width // per
    half = DH // 2
    blocks = GROUP // 2 + 1
    span = blocks * PAIR
    before = sum(sizes)
    wide = before + rows
    edges = [sum(sizes[:p]) for p in range(hist + 1)] + [wide]

    def get_x():
        return pltpu.make_async_copy(x_hbm, x_ref, sems.at[0])

    def get_acc(g):
        at = pl.ds(pl.multiple_of(g * span, PAIR), span)
        src = acc_hbm.at[at, pl.ds(start, rows)]
        return pltpu.make_async_copy(src, acc_ref.at[at], sems.at[1 + g])

    def get_w(g, j):
        at = pl.ds(pl.multiple_of(g * span, PAIR), span)
        src = w_hbm.at[which_ref[0], j, at]
        return pltpu.make_async_copy(src, w_ref.at[j, at], sems.at[1 + groups + g * per + j])

    get_x().start()
    for g in range(groups):
        for j in range(per):
            get_w(g, j).start()
        get_acc(g).start()

    key = start - before + lax.broadcasted_iota(jnp.int32, (wide, rows), 0)
    tok = start + lax.broadcasted_iota(jnp.int32, (wide, rows), 1)
    bias[...] = jnp.where((key <= tok) & (key >= begin_ref[...]), 0.0, -1e30)
    last = gain_ref.shape[0] - 1

    def put(r, m, y):
        xn[pl.ds(r, m), :] = y

    get_x().wait()
    normalise(x_ref, inv_ref, gain_ref[last : last + 1, :], rows, 0, put)

    def rotary(u):
        a, b = u[:half], u[half:]
        c, s = cos_ref[...], sin_ref[...]
        return jnp.concatenate([a * c - b * s, b * c + a * s], axis=0)

    def project(at):
        total = acc_ref[at, :]
        for j in range(per):
            total = total + dot(w_ref[j, at, :], xn[:, j * f2 : (j + 1) * f2], NT)
        return total

    @pl.loop(0, groups)
    def _(g):
        for j in range(per):
            get_w(g, j).wait()
        get_acc(g).wait()
        base = g * span
        total = project(pl.ds(pl.multiple_of(base + (blocks - 1) * PAIR, PAIR), PAIR))
        k_ref[g] = rotary(total[:DH]).T.astype(BF16)
        v_ref[g] = total[DH:].astype(BF16)

        for i in range(blocks - 1):
            total = project(pl.ds(pl.multiple_of(base + i * PAIR, PAIR), PAIR))
            for h in range(2):
                q = rotary(total[h * DH : (h + 1) * DH]).astype(BF16)
                scores = []
                for p in range(hist + 1):
                    src = keys[p] if p < hist else k_ref
                    s = dot(src[g], q, NN) * (math.log2(math.e) / math.sqrt(DH))
                    scores.append(s + bias[edges[p] : edges[p + 1], :])
                top = scores[0].max(axis=0, keepdims=True)
                for s in scores[1:]:
                    top = jnp.maximum(top, s.max(axis=0, keepdims=True))
                expo = [jnp.exp2(s - top) for s in scores]
                norm = expo[0].sum(axis=0, keepdims=True)
                for e in expo[1:]:
                    norm = norm + e.sum(axis=0, keepdims=True)
                scale = 1.0 / norm
                out = None
                for p in range(hist + 1):
                    src = values[p] if p < hist else v_ref
                    part = dot(src[g], expo[p].astype(BF16), NN)
                    out = part if out is None else out + part
                at = pl.multiple_of((g * (blocks - 1) + i) * PAIR + h * DH, DH)
                out_ref[:, pl.ds(at, DH)] = (out * scale).T.astype(BF16)


def late(start, which, x, inv, gains, whole, per, acc, cos, sin, begin, past, out):
    rows, width = x.shape
    cols, count = acc.shape
    c = start // rows
    w4 = whole.reshape(-1, per, cols, whole.shape[2])
    sizes = tuple(k.shape[1] for k, _ in past)
    groups = cols // DH // (GROUP + 2)
    heads = groups * GROUP
    aliased = 0 if out is None else 1
    wide = sum(sizes) + rows

    grid = pltpu.PrefetchScalarGridSpec(
        num_scalar_prefetch=1,
        grid=(1,),
        in_specs=[
            pl.BlockSpec((rows, 1), lambda n, f: (c, 0)),
            pl.BlockSpec(gains.shape, lambda n, f: (0, 0)),
            pl.BlockSpec((DH // 2, rows), lambda n, f: (0, c)),
            pl.BlockSpec((DH // 2, rows), lambda n, f: (0, c)),
            pl.BlockSpec((1, rows), lambda n, f: (0, c)),
        ]
        + [pl.BlockSpec((groups, r, DH), lambda n, f: (0, 0, 0)) for r in sizes]
        + [pl.BlockSpec((groups, DH, r), lambda n, f: (0, 0, 0)) for r in sizes]
        + [any_spec()] * (3 + aliased),
        out_specs=[
            pl.BlockSpec((rows, heads * DH), lambda n, f: (c, 0)),
            pl.BlockSpec((groups, rows, DH), lambda n, f: (0, 0, 0)),
            pl.BlockSpec((groups, DH, rows), lambda n, f: (0, 0, 0)),
        ],
        scratch_shapes=[
            pltpu.VMEM((rows, width), BF16),
            pltpu.VMEM((per, cols, whole.shape[2]), BF16),
            pltpu.VMEM((cols, rows), F32),
            pltpu.VMEM((rows, width), BF16),
            pltpu.VMEM((wide, rows), F32),
            pltpu.SemaphoreType.DMA((1 + groups + groups * per,)),
        ],
    )
    return pl.pallas_call(
        functools.partial(late_kernel, start, sizes, per, groups, aliased),
        grid_spec=grid,
        out_shape=(
            jax.ShapeDtypeStruct((count, heads * DH), BF16),
            jax.ShapeDtypeStruct((groups, rows, DH), BF16),
            jax.ShapeDtypeStruct((groups, DH, rows), BF16),
        ),
        input_output_aliases={9 + 2 * len(sizes): 0} if aliased else {},
        compiler_params=params(),
        cost_estimate=pl.CostEstimate(
            flops=2 * rows * width * cols + 4 * rows * wide * DH * heads,
            bytes_accessed=width * cols * 2 + rows * cols * 4 + rows * heads * DH * 2,
            transcendentals=rows * wide * heads,
        ),
        name="late",
    )(
        which, inv, gains, cos, sin, begin,
        *[k for k, _ in past], *[v for _, v in past], x, w4, acc, *([out] if aliased else []),
    )


def cut_kernel(first, size, x_hbm, o_ref, sem):
    copy = pltpu.make_async_copy(x_hbm.at[pl.ds(first, size)], o_ref, sem)
    copy.start()
    copy.wait()


def cut(x, first, size):
    return pl.pallas_call(
        functools.partial(cut_kernel, first, size),
        in_specs=[any_spec()],
        out_specs=pl.BlockSpec(memory_space=pltpu.VMEM),
        out_shape=jax.ShapeDtypeStruct((size, x.shape[1]), x.dtype),
        scratch_shapes=[pltpu.SemaphoreType.DMA],
        compiler_params=params(60),
        name="cut",
    )(x)


def shards(axes, tokens, norm_gain, weights_gen, segment_ids):
    return layer(axes, tokens, norm_gain, weights_gen, segment_ids)


def layer(axes, tokens, norm_gain, weights_gen, segment_ids):
    tp, pp = axes["tp"], axes["pp"]
    count, width = tokens.shape
    groups, qrows, f2 = weights_gen.shape
    per = width // f2
    chunks = CHUNKS
    rows = count // chunks
    me = lax.axis_index("pp")
    z = lax.axis_index("tp")

    ring = [(i, (i - 1) % tp) for i in range(tp)]
    first = cut(tokens, 0, rows)
    rest, first = lax.optimization_barrier((tokens, first))
    step = [first] + [rest[c * rows : (c + 1) * rows] for c in range(1, chunks)]
    got = []
    for k in range(1, tp):
        step = [lax.ppermute(step[c], "tp", ring) for c in range(chunks)]
        got.append(step)

    flat = weights_gen.reshape(groups * qrows, f2)
    part = flat.shape[0] // 2

    def swap(x, mask):
        return lax.ppermute(x, "pp", [(i, i ^ mask) for i in range(pp)])

    def half_of(h):
        return cut(flat, h * part, part)

    slices = {0: [half_of(h) for h in range(2)]}
    order = sorted(range(2, pp, 2), key=lambda m: (bin(m).count("1"), m))
    for m in order:
        bits = [1 << b for b in range(pp.bit_length()) if m >> b & 1]
        via = [bits[0], bits[-1]]
        slices[m] = [swap(slices[m ^ via[h]][h], via[h]) for h in range(2)]
    for m in [0] + order:
        slices[m | 1] = [swap(s, 1) for s in slices[m]]

    floats = rest.astype(F32)
    small = jnp.concatenate([jnp.sum(floats * floats, axis=1), norm_gain.astype(F32)])
    small = small.reshape(-1, 128)
    smalls = [small]
    for k in range(1, tp):
        smalls.append(lax.ppermute(smalls[-1], "tp", ring))
    smalls = [s.reshape(-1) for s in smalls]
    square = sum(s[:count] for s in smalls) / (tp * width)
    inv = lax.rsqrt(square + 1e-05)[:, None]
    gains = jnp.stack([s[count:] for s in smalls])
    which = (z + jnp.arange(tp, dtype=jnp.int32)) % tp
    far = (me ^ (pp - 2)) // per
    step_far = (far - z) % tp
    half_steps = tp // 2
    near = jnp.arange(half_steps, dtype=jnp.int32)
    units1 = jnp.concatenate([near, which[:half_steps], near != step_far]).astype(jnp.int32)
    late_steps = jnp.arange(half_steps, tp - 1, dtype=jnp.int32)
    waits = step_far < half_steps
    early_far = jnp.where(waits, step_far, 0)[None]
    units2 = jnp.concatenate(
        [early_far, late_steps, (z + early_far) % tp, which[half_steps : tp - 1], waits[None], late_steps >= 0]
    ).astype(jnp.int32)

    seg = segment_ids[0]
    begin = jnp.sum((seg[None, :] < seg[:, None]).astype(jnp.int32), axis=1)
    positions = jnp.arange(count, dtype=jnp.int32) - begin
    half = DH // 2
    freq = jnp.exp(jnp.arange(half, dtype=F32) * (-2.0 * math.log(rope_base) / DH))
    angle = freq[:, None] * positions.astype(F32)[None, :]
    cos, sin = jnp.cos(angle), jnp.sin(angle)

    levels = range(max(bin(m).count("1") for m in order) + 1)
    stages = []
    for n in levels:
        here = [m for m in [0] + order if bin(m).count("1") == n]
        if n == 0:
            stages.append([(m | b, h) for m in here for b in range(2) for h in range(2)])
        elif n < levels[-1]:
            stages += [[(m | b, h) for m in here for b in range(2)] for h in range(2)]
        else:
            stages += [[(m | b, h) for m in here for h in range(2)] for b in range(2)]
    state = None
    xs = None
    acc = None
    for n, stage in enumerate(stages):
        masks = sorted({m for m, _ in stage})
        items = [(masks.index(m), h * part, slices[m][h]) for m, h in stage]
        where = jnp.concatenate([me[None], me ^ jnp.array(masks, jnp.int32)]).astype(jnp.int32)
        if n == len(stages) - 2:
            xs = prep(0, 0, tokens, inv, gains, None)
            for k in range(1, half_steps):
                for c in range(chunks):
                    xs = prep(k, c * rows, got[k - 1][c], inv, gains, xs)
            xs, cos, sin, inv, gains, units1, units2, which = lax.optimization_barrier(
                (xs, cos, sin, inv, gains, units1, units2, which)
            )
            acc = early(half_steps, units1, xs, state[0], per, None)
        state = place(state, where, items, groups * qrows, groups, pp)
    whole, weights_rows = state
    for k in range(half_steps, tp - 1):
        for c in range(chunks):
            xs = prep(k, c * rows, got[k - 1][c], inv, gains, xs)
    acc = early(tp - half_steps, units2, xs, whole, per, acc)

    out, past = None, []
    for c in range(chunks):
        near = [kv for at, kv in past if at + rows > c * rows - SPAN + 1]
        out, k, v = late(
            c * rows, which[tp - 1 :], got[-1][c], inv, gains, whole, per, acc, cos, sin,
            begin[None, :], near, out,
        )
        past.append((c * rows, (k, v)))
    return weights_rows, out


def solution(mesh):
    in_specs = (P("pp", "tp"), P("tp"), P("tp", None, "pp"), P("pp", None))
    out_specs = (P("tp", "pp", None), P("pp", "tp"))
    axes = dict(mesh.shape)
    body = functools.partial(shards, axes)
    return jax.shard_map(body, mesh=mesh, in_specs=in_specs, out_specs=out_specs, check_vma=False)
```

time: 659 us -> 474 us (0.72)
  the two profiles are of different devices: /device:TPU:0 before, /device:TPU:10 now
where the time goes in v1:
time: 474 us; the launch traced here: 473 us
  waiting for transfers between devices  203 us (43%)
  Pallas kernels  200 us (42%)
  starting transfers between devices  46.6 us (10%)
  local copies, waits for them, and re-layouts  13.3 us (3%)
  other arithmetic  9.39 us (2%)
    ppermute x14, waiting for transfers between devices, swap(): return lax.ppermute(x, 'pp', [(i, i ^ mask) for i in range(pp)])  112 us
    pallas_call x4, Pallas kernels, late(): pl.pallas_call(functools.partial(late_kernel, start, sizes, per, groups,...  68.1 us
    pallas_call x2, Pallas kernels, early(): pl.pallas_call(functools.partial(early_kernel, units, per, old), grid_spe...  55.8 us
    ppermute x12, waiting for transfers between devices, layer(): step = [lax.ppermute(step[c], 'tp', ring) for c in range(chunks)]  48.8 us
    ppermute x3, waiting for transfers between devices, layer(): smalls.append(lax.ppermute(smalls[-1], 'tp', ring))  42.4 us
    pallas_call x5, Pallas kernels, place(): pl.pallas_call(functools.partial(place_kernel, pieces, old, groups, slice...  38.8 us
    ppermute x12, starting transfers between devices, layer(): step = [lax.ppermute(step[c], 'tp', ring) for c in range(chunks)]  34.8 us
    pallas_call x9, Pallas kernels, prep(): pl.pallas_call(functools.partial(prep_kernel, k), grid=(rows // block,),...  28.3 us
  transfers between devices with their start and end apart: 29, of which 9 were waited for; matrix products, arithmetic and copies ran while one was open for 4% of the time, Pallas kernels for 38%

profile of v1, /device:TPU:10, one launch (start us, length us, event | category | flops | bytes accessed | tf_op | source)
XLA Modules:
  0.0 472.8 jit_solution(12431439030163605136)
XLA Ops:
  8.3 3.8 fusion.1
  17.1 38.9 %collective-permute-done.15 = f32[24,128]{1,0:T(8,128)S(1)} collective-permute-done((f32[24,128]{1,0:T(8,128)S(1)}, f32[24,128]{1,0:T(8,128)S(1)}, u32[]{:S(2)}, u32[]{:S(2)}) %collective-permute-start.15) | collective-permute-done | bytes 12320 | tf_op jit(solution)/shard_map/ppermute | solution.py:459
  59.7 3.6 collective-permute-start.17
  64.7 4.1 collective-permute-start.18
  68.8 4.1 collective-permute-start.14
  76.7 15.9 %collective-permute-done.18.x_ref = bf16[256,2048]{1,0:T(8,128)(2,1)S(1)} collective-permute-done((bf16[256,2048]{1,0:T(8,128)(2,1)}, bf16[256,2048]{1,0:T(8,128)(2,1)S(1)}, u32[]{:S(2)}, u32[]{:S(2)}) %collective-permute-start.18) | collective-permute-done | bytes 1048608 | tf_op jit(solution)/shard_map/ppermute | solution.py:433
  92.6 19.0 %collective-permute-done.14.x_ref = bf16[256,2048]{1,0:T(8,128)(2,1)} collective-permute-done((bf16[256,2048]{1,0:T(8,128)(2,1)}, bf16[256,2048]{1,0:T(8,128)(2,1)}, u32[]{:S(2)}, u32[]{:S(2)}) %collective-permute-start.14) | collective-permute-done | bytes 1048608 | tf_op jit(solution)/shard_map/ppermute | solution.py:433
  113.1 19.8 %collective-permute-done.9.refs_0_ = bf16[1280,1024]{1,0:T(8,128)(2,1)} collective-permute-done((bf16[1280,1024]{1,0:T(8,128)(2,1)S(1)}, bf16[1280,1024]{1,0:T(8,128)(2,1)}, u32[]{:S(2)}, u32[]{:S(2)}) %collective-permute-start.9) | collective-permute-done | bytes 2621472 | tf_op jit(solution)/shard_map/ppermute | solution.py:440
  133.4 55.6 %collective-permute-done.3.refs_0_ = bf16[1280,1024]{1,0:T(8,128)(2,1)} collective-permute-done((bf16[1280,1024]{1,0:T(8,128)(2,1)}, bf16[1280,1024]{1,0:T(8,128)(2,1)}, u32[]{:S(2)}, u32[]{:S(2)}) %collective-permute-start.3) | collective-permute-done | bytes 2621472 | tf_op jit(solution)/shard_map/ppermute | solution.py:440
  204.6 36.1 %collective-permute-done.1.refs_0_ = bf16[1280,1024]{1,0:T(8,128)(2,1)} collective-permute-done((bf16[1280,1024]{1,0:T(8,128)(2,1)}, bf16[1280,1024]{1,0:T(8,128)(2,1)}, u32[]{:S(2)}, u32[]{:S(2)}) %collective-permute-start.1) | collective-permute-done | bytes 2621472 | tf_op jit(solution)/shard_map/ppermute | solution.py:440
  241.9 5.8 %prep.9.refs_0_ = bf16[3,1024,2048]{2,1,0:T(8,128)(2,1)} custom-call(bf16[1024,2048]{1,0:T(8,128)(2,1)} %x_ref.1, f32[1024,1]{1,0:T(8,128)} %add_rsqrt_fusion.inv_ref, f32[4,2048]{1,0:T(4,128)} %pad_maximum_fusion.gain_ref), custom_call_target="tpu_custom_call" | custom-call | flops 209715200 | bytes 8388608 | tf_op jit(solution)/shard_map/prep/pallas_call | solution.py:148
  259.6 9.5 %place.5 = (bf16[8,2560,1024]{2,1,0:T(8,128)(2,1)}, bf16[2,160,8192]{2,1,0:T(8,128)(2,1)}) custom-call(s32[3]{0:T(128)} %pad_add_fusion.3.where_ref, bf16[1280,1024]{1,0:T(8,128)(2,1)} %cut.3.refs_0_, bf16[1280,1024]{1,0:T(8,128)(2,1)} %cut.4.refs_1_, bf16[1280,1024]{1,0:T(8,128)(2,1)} %collective-permute-done.12.refs_2_, bf16[1280,1024]{1,0:T(8,128)(2,1)} %copy-done.3), custom_call_target="tpu_custom_call" | custom-call | flops 1048576000 | bytes 20971520 | tf_op jit(solution)/shard_map/place/pallas_call | solution.py:120
  269.1 9.7 %place.6 = (bf16[8,2560,1024]{2,1,0:T(8,128)(2,1)}, bf16[2,160,8192]{2,1,0:T(8,128)(2,1)}) custom-call(s32[5]{0:T(128)} %pad_add_fusion.2.where_ref, bf16[1280,1024]{1,0:T(8,128)(2,1)} %collective-permute-done.9.refs_0_, bf16[1280,1024]{1,0:T(8,128)(2,1)} %collective-permute-done.10.refs_1_, ...), custom_call_target="tpu_custom_call", output_to_operand_aliasing={{0}: (5, {}), {1}: (6, {})} | custom-call | flops 1048576000 | bytes 20971520 | tf_op jit(solution)/shard_map/place/pallas_call | solution.py:120
  280.3 9.5 %place.7 = (bf16[8,2560,1024]{2,1,0:T(8,128)(2,1)}, bf16[2,160,8192]{2,1,0:T(8,128)(2,1)}) custom-call(s32[5]{0:T(128)} %pad_add_fusion.2.where_ref, bf16[1280,1024]{1,0:T(8,128)(2,1)} %collective-permute-done.3.refs_0_, bf16[1280,1024]{1,0:T(8,128)(2,1)} %copy-done.2, ...), custom_call_target="tpu_custom_call", output_to_operand_aliasing={{0}: (5, {}), {1}: (6, {})} | custom-call | flops 1048576000 | bytes 20971520 | tf_op jit(solution)/shard_map/place/pallas_call | solution.py:120
  291.1 21.0 %early.2.refs_2_ = f32[2560,1024]{1,0:T(8,128)} custom-call(s32[6]{0:T(128)} %pad_add_fusion.4.which_ref, bf16[3,1024,2048]{2,1,0:T(8,128)(2,1)} %prep.13.refs_0_.x_hbm, bf16[4,2,2560,1024]{3,2,1,0:T(8,128)(2,1)} %bitcast.20, bf16[4,2,2560,1024]{3,2,1,0:T(8,128)(2,1)} %bitcast.21), custom_call_target="tpu_custom_call" | custom-call | flops 21474836480 | bytes 39845888 | tf_op jit(solution)/shard_map/early/pallas_call | solution.py:228
  314.9 14.7 %collective-permute-start.22 = (bf16[256,2048]{1,0:T(8,128)(2,1)}, bf16[256,2048]{1,0:T(8,128)(2,1)}, u32[]{:S(2)}, u32[]{:S(2)}) collective-permute-start(bf16[256,2048]{1,0:T(8,128)(2,1)} %collective-permute-done.21.x_ref), channel_id=1, source_target_pairs={{0,24},{8,0},{16,8},{24,16},{1,25},{9,1},{17,9},{25,17},{2,26},{10... | collective-permute-start | bytes 3145736 | tf_op jit(solution)/shard_map/ppermute | solution.py:433
  336.3 14.0 %collective-permute-done.23.x_ref = bf16[256,2048]{1,0:T(8,128)(2,1)} collective-permute-done((bf16[256,2048]{1,0:T(8,128)(2,1)}, bf16[256,2048]{1,0:T(8,128)(2,1)}, u32[]{:S(2)}, u32[]{:S(2)}) %collective-permute-start.23) | collective-permute-done | bytes 1048608 | tf_op jit(solution)/shard_map/ppermute | solution.py:433
  354.1 5.0 %place.8 = (bf16[8,2560,1024]{2,1,0:T(8,128)(2,1)}, bf16[2,160,8192]{2,1,0:T(8,128)(2,1)}) custom-call(s32[2]{0:T(128)} %pad_add_fusion.1.where_ref, bf16[1280,1024]{1,0:T(8,128)(2,1)} %collective-permute-done.1.refs_0_, bf16[1280,1024]{1,0:T(8,128)(2,1)} %collective-permute-done.4.refs_1_, ...), custom_call_target="tpu_custom_call", output_to_operand_aliasing={{0}: (3, {}), {1}: (4, {})} | custom-call | flops 524288000 | bytes 10485760 | tf_op jit(solution)/shard_map/place/pallas_call | solution.py:120
  361.5 5.0 %place.9 = (bf16[8,2560,1024]{2,1,0:T(8,128)(2,1)}, bf16[2,160,8192]{2,1,0:T(8,128)(2,1)}) custom-call(s32[2]{0:T(128)} %pad_add_fusion.where_ref, bf16[1280,1024]{1,0:T(8,128)(2,1)} %collective-permute-done.2.refs_0_, bf16[1280,1024]{1,0:T(8,128)(2,1)} %collective-permute-done.5.refs_1_, ...), custom_call_target="tpu_custom_call", output_to_operand_aliasing={{0}: (3, {}), {1}: (4, {})} | custom-call | flops 524288000 | bytes 10485760 | tf_op jit(solution)/shard_map/place/pallas_call | solution.py:120
  366.5 34.9 %early.3.refs_2_.refs_4_.refs_6_ = f32[2560,1024]{1,0:T(8,128)} custom-call(s32[6]{0:T(128)} %concatenate.31.which_ref, bf16[3,1024,2048]{2,1,0:T(8,128)(2,1)} %prep.17.x_hbm, bf16[4,2,2560,1024]{3,2,1,0:T(8,128)(2,1)} %bitcast.22, bf16[4,2,2560,1024]{3,2,1,0:T(8,128)(2,1)} %bitcast.23, f32[2560,1024]{1,0:T(8,128)} %early.2.refs_2_), custom_call_target="tpu_custom_call", output_to_operand_aliasing={{}: (4, {})} | custom-call | flops 21474836480 | bytes 50331648 | tf_op jit(solution)/shard_map/early/pallas_call | solution.py:228
  401.4 14.1 %late.4 = (bf16[1024,2048]{1,0:T(8,128)(2,1)}, bf16[2,256,128]{2,1,0:T(8,128)(2,1)}, bf16[2,128,256]{2,1,0:T(8,128)(2,1)}) custom-call(s32[1]{0:T(128)} %slice.65.which_ref, f32[1024,1]{1,0:T(8,128)} %add_rsqrt_fusion.inv_ref, f32[4,2048]{1,0:T(4,128)} %pad_maximum_fusion.gain_ref, f32[64,1024]{1,0:T(8,128)} %get-tuple-element.46.cos_ref, ...), custom_call_target="tpu_custom_call" | custom-call | flops 3221225472 | bytes 14155776 | tf_op jit(solution)/shard_map/late/pallas_call | solution.py:373
  416.6 17.9 %late.5 = (bf16[1024,2048]{1,0:T(8,128)(2,1)}, bf16[2,256,128]{2,1,0:T(8,128)(2,1)}, bf16[2,128,256]{2,1,0:T(8,128)(2,1)}) custom-call(s32[1]{0:T(128)} %slice.65.which_ref, f32[1024,1]{1,0:T(8,128)} %add_rsqrt_fusion.inv_ref, f32[4,2048]{1,0:T(4,128)} %pad_maximum_fusion.gain_ref, ...), custom_call_target="tpu_custom_call", output_to_operand_aliasing={{0}: (11, {})} | custom-call | flops 3758096384 | bytes 14155776 | tf_op jit(solution)/shard_map/late/pallas_call | solution.py:373
  435.5 18.1 %late.6 = (bf16[1024,2048]{1,0:T(8,128)(2,1)}, bf16[2,256,128]{2,1,0:T(8,128)(2,1)}, bf16[2,128,256]{2,1,0:T(8,128)(2,1)}) custom-call(s32[1]{0:T(128)} %slice.65.which_ref, f32[1024,1]{1,0:T(8,128)} %add_rsqrt_fusion.inv_ref, f32[4,2048]{1,0:T(4,128)} %pad_maximum_fusion.gain_ref, ...), custom_call_target="tpu_custom_call", output_to_operand_aliasing={{0}: (13, {})} | custom-call | flops 4294967296 | bytes 14155776 | tf_op jit(solution)/shard_map/late/pallas_call | solution.py:373
  454.5 18.1 %late.7 = (bf16[1024,2048]{1,0:T(8,128)(2,1)}, bf16[2,256,128]{2,1,0:T(8,128)(2,1)}, bf16[2,128,256]{2,1,0:T(8,128)(2,1)}) custom-call(s32[1]{0:T(128)} %slice.65.which_ref, f32[1024,1]{1,0:T(8,128)} %add_rsqrt_fusion.inv_ref, f32[4,2048]{1,0:T(4,128)} %pad_maximum_fusion.gain_ref, ...), custom_call_target="tpu_custom_call", output_to_operand_aliasing={{0}: (13, {})} | custom-call | flops 4294967296 | bytes 14155776 | tf_op jit(solution)/shard_map/late/pallas_call | solution.py:373
  (118 shorter events, 73.6 us)
Async XLA Ops:
  3.9 108.3 %collective-permute-start.12 = (bf16[1280,1024]{1,0:T(8,128)(2,1)}, bf16[1280,1024]{1,0:T(8,128)(2,1)}, u32[]{:S(2)}, u32[]{:S(2)}) collective-permute-start(bf16[1280,1024]{1,0:T(8,128)(2,1)} %cut.3.refs_0_), channel_id=1, source_target_pairs={{0,1},{1,0},{2,3},{3,2},{4,5},{5,4},{6,7},{7,6},{8,9},{9,8},{10,11... | collective-permute-start | bytes 7864328 | tf_op jit(solution)/shard_map/ppermute | solution.py:440
  4.0 109.1 %collective-permute-start = (bf16[1280,1024]{1,0:T(8,128)(2,1)}, bf16[1280,1024]{1,0:T(8,128)(2,1)}, u32[]{:S(2)}, u32[]{:S(2)}) collective-permute-start(bf16[1280,1024]{1,0:T(8,128)(2,1)} %cut.3.refs_0_), channel_id=1, source_target_pairs={{0,4},{1,5},{2,6},{3,7},{4,0},{5,1},{6,2},{7,3},{8,12},{9,13},{10,... | collective-permute-start | bytes 7864328 | tf_op jit(solution)/shard_map/ppermute | solution.py:440
  7.8 61.0 %collective-permute-start.20 = (bf16[256,2048]{1,0:T(8,128)(2,1)}, bf16[256,2048]{1,0:T(8,128)(2,1)S(1)}, u32[]{:S(2)}, u32[]{:S(2)}) collective-permute-start(bf16[256,2048]{1,0:T(8,128)(2,1)} %cut.5), channel_id=1, source_target_pairs={{0,24},{8,0},{16,8},{24,16},{1,25},{9,1},{17,9},{25,17},{2,26},{10... | collective-permute-start | bytes 3145736 | tf_op jit(solution)/shard_map/ppermute | solution.py:433
  12.1 60.8 %collective-permute-start.19 = (bf16[256,2048]{1,0:T(8,128)(2,1)S(1)}, bf16[256,2048]{1,0:T(8,128)(2,1)}, u32[]{:S(2)}, u32[]{:S(2)}) collective-permute-start(bf16[256,2048]{1,0:T(8,128)(2,1)S(1)} %get-tuple-element.62), channel_id=1, source_target_pairs={{0,24},{8,0},{16,8},{24,16},{1,25},{9,1},{17,9},{25,17},{2,26},{10... | collective-permute-start | bytes 3145736 | tf_op jit(solution)/shard_map/ppermute | solution.py:433
  68.8 42.8 %collective-permute-start.14 = (bf16[256,2048]{1,0:T(8,128)(2,1)}, bf16[256,2048]{1,0:T(8,128)(2,1)}, u32[]{:S(2)}, u32[]{:S(2)}) collective-permute-start(bf16[256,2048]{1,0:T(8,128)(2,1)} %get-tuple-element.64), channel_id=1, source_target_pairs={{0,24},{8,0},{16,8},{24,16},{1,25},{9,1},{17,9},{25,17},{2,26},{10... | collective-permute-start | bytes 3145736 | tf_op jit(solution)/shard_map/ppermute | solution.py:433
  72.9 59.9 %collective-permute-start.9 = (bf16[1280,1024]{1,0:T(8,128)(2,1)S(1)}, bf16[1280,1024]{1,0:T(8,128)(2,1)}, u32[]{:S(2)}, u32[]{:S(2)}) collective-permute-start(bf16[1280,1024]{1,0:T(8,128)(2,1)S(1)} %copy-done.1), channel_id=1, source_target_pairs={{0,2},{1,3},{2,0},{3,1},{4,6},{5,7},{6,4},{7,5},{8,10},{9,11},{10,... | collective-permute-start | bytes 7864328 | tf_op jit(solution)/shard_map/ppermute | solution.py:440
  92.6 40.2 %collective-permute-start.13 = (bf16[1280,1024]{1,0:T(8,128)(2,1)}, bf16[1280,1024]{1,0:T(8,128)(2,1)S(1)}, u32[]{:S(2)}, u32[]{:S(2)}) collective-permute-start(bf16[1280,1024]{1,0:T(8,128)(2,1)} %cut.4.refs_1_), channel_id=1, source_target_pairs={{0,1},{1,0},{2,3},{3,2},{4,5},{5,4},{6,7},{7,6},{8,9},{9,8},{10,11... | collective-permute-start | bytes 7864328 | tf_op jit(solution)/shard_map/ppermute | solution.py:440
  111.6 77.4 %collective-permute-start.3 = (bf16[1280,1024]{1,0:T(8,128)(2,1)}, bf16[1280,1024]{1,0:T(8,128)(2,1)}, u32[]{:S(2)}, u32[]{:S(2)}) collective-permute-start(bf16[1280,1024]{1,0:T(8,128)(2,1)} %cut.4.refs_1_), channel_id=1, source_target_pairs={{0,2},{1,3},{2,0},{3,1},{4,6},{5,7},{6,4},{7,5},{8,10},{9,11},{10,... | collective-permute-start | bytes 7864328 | tf_op jit(solution)/shard_map/ppermute | solution.py:440
  112.1 77.4 %collective-permute-start.7 = (bf16[1280,1024]{1,0:T(8,128)(2,1)}, bf16[1280,1024]{1,0:T(8,128)(2,1)}, u32[]{:S(2)}, u32[]{:S(2)}) collective-permute-start(bf16[1280,1024]{1,0:T(8,128)(2,1)} %cut.4.refs_1_), channel_id=1, source_target_pairs={{0,4},{1,5},{2,6},{3,7},{4,0},{5,1},{6,2},{7,3},{8,12},{9,13},{10,... | collective-permute-start | bytes 7864328 | tf_op jit(solution)/shard_map/ppermute | solution.py:440
  113.1 76.5 %collective-permute-start.11 = (bf16[1280,1024]{1,0:T(8,128)(2,1)}, bf16[1280,1024]{1,0:T(8,128)(2,1)}, u32[]{:S(2)}, u32[]{:S(2)}) collective-permute-start(bf16[1280,1024]{1,0:T(8,128)(2,1)} %collective-permute-done.refs_2_), channel_id=1, source_target_pairs={{0,1},{1,0},{2,3},{3,2},{4,5},{5,4},{6,7},{7,6},{8,9},{9,8},{10,11... | collective-permute-start | bytes 7864328 | tf_op jit(solution)/shard_map/ppermute | solution.py:440
  132.8 63.7 %collective-permute-start.10 = (bf16[1280,1024]{1,0:T(8,128)(2,1)}, bf16[1280,1024]{1,0:T(8,128)(2,1)}, u32[]{:S(2)}, u32[]{:S(2)}) collective-permute-start(bf16[1280,1024]{1,0:T(8,128)(2,1)} %collective-permute-done.9.refs_0_), channel_id=1, source_target_pairs={{0,1},{1,0},{2,3},{3,2},{4,5},{5,4},{6,7},{7,6},{8,9},{9,8},{10,11... | collective-permute-start | bytes 7864328 | tf_op jit(solution)/shard_map/ppermute | solution.py:440
  132.8 107.9 %collective-permute-start.1 = (bf16[1280,1024]{1,0:T(8,128)(2,1)}, bf16[1280,1024]{1,0:T(8,128)(2,1)}, u32[]{:S(2)}, u32[]{:S(2)}) collective-permute-start(bf16[1280,1024]{1,0:T(8,128)(2,1)} %collective-permute-done.refs_2_), channel_id=1, source_target_pairs={{0,2},{1,3},{2,0},{3,1},{4,6},{5,7},{6,4},{7,5},{8,10},{9,11},{10,... | collective-permute-start | bytes 7864328 | tf_op jit(solution)/shard_map/ppermute | solution.py:440
  189.0 51.8 %collective-permute-start.4 = (bf16[1280,1024]{1,0:T(8,128)(2,1)}, bf16[1280,1024]{1,0:T(8,128)(2,1)}, u32[]{:S(2)}, u32[]{:S(2)}) collective-permute-start(bf16[1280,1024]{1,0:T(8,128)(2,1)} %collective-permute-done.3.refs_0_), channel_id=1, source_target_pairs={{0,4},{1,5},{2,6},{3,7},{4,0},{5,1},{6,2},{7,3},{8,12},{9,13},{10,... | collective-permute-start | bytes 7864328 | tf_op jit(solution)/shard_map/ppermute | solution.py:440
  189.5 89.3 %collective-permute-start.6 = (bf16[1280,1024]{1,0:T(8,128)(2,1)}, bf16[1280,1024]{1,0:T(8,128)(2,1)S(1)}, u32[]{:S(2)}, u32[]{:S(2)}) collective-permute-start(bf16[1280,1024]{1,0:T(8,128)(2,1)} %collective-permute-done.3.refs_0_), channel_id=1, source_target_pairs={{0,1},{1,0},{2,3},{3,2},{4,5},{5,4},{6,7},{7,6},{8,9},{9,8},{10,11... | collective-permute-start | bytes 7864328 | tf_op jit(solution)/shard_map/ppermute | solution.py:440
  189.6 90.4 %collective-permute-start.8 = (bf16[1280,1024]{1,0:T(8,128)(2,1)}, bf16[1280,1024]{1,0:T(8,128)(2,1)}, u32[]{:S(2)}, u32[]{:S(2)}) collective-permute-start(bf16[1280,1024]{1,0:T(8,128)(2,1)} %collective-permute-done.7.refs_2_), channel_id=1, source_target_pairs={{0,1},{1,0},{2,3},{3,2},{4,5},{5,4},{6,7},{7,6},{8,9},{9,8},{10,11... | collective-permute-start | bytes 7864328 | tf_op jit(solution)/shard_map/ppermute | solution.py:440
  196.5 93.4 %collective-permute-start.21 = (bf16[256,2048]{1,0:T(8,128)(2,1)}, bf16[256,2048]{1,0:T(8,128)(2,1)}, u32[]{:S(2)}, u32[]{:S(2)}) collective-permute-start(bf16[256,2048]{1,0:T(8,128)(2,1)} %copy-done.7), channel_id=1, source_target_pairs={{0,24},{8,0},{16,8},{24,16},{1,25},{9,1},{17,9},{25,17},{2,26},{10... | collective-permute-start | bytes 3145736 | tf_op jit(solution)/shard_map/ppermute | solution.py:433
  240.8 118.4 %collective-permute-start.2 = (bf16[1280,1024]{1,0:T(8,128)(2,1)}, bf16[1280,1024]{1,0:T(8,128)(2,1)}, u32[]{:S(2)}, u32[]{:S(2)}) collective-permute-start(bf16[1280,1024]{1,0:T(8,128)(2,1)} %collective-permute-done.1.refs_0_), channel_id=1, source_target_pairs={{0,1},{1,0},{2,3},{3,2},{4,5},{5,4},{6,7},{7,6},{8,9},{9,8},{10,11... | collective-permute-start | bytes 7864328 | tf_op jit(solution)/shard_map/ppermute | solution.py:440
  240.8 120.7 %collective-permute-start.5 = (bf16[1280,1024]{1,0:T(8,128)(2,1)}, bf16[1280,1024]{1,0:T(8,128)(2,1)}, u32[]{:S(2)}, u32[]{:S(2)}) collective-permute-start(bf16[1280,1024]{1,0:T(8,128)(2,1)} %collective-permute-done.4.refs_1_), channel_id=1, source_target_pairs={{0,1},{1,0},{2,3},{3,2},{4,5},{5,4},{6,7},{7,6},{8,9},{9,8},{10,11... | collective-permute-start | bytes 7864328 | tf_op jit(solution)/shard_map/ppermute | solution.py:440
  280.0 52.3 %collective-permute-start.24 = (bf16[256,2048]{1,0:T(8,128)(2,1)S(1)}, bf16[256,2048]{1,0:T(8,128)(2,1)}, u32[]{:S(2)}, u32[]{:S(2)}) collective-permute-start(bf16[256,2048]{1,0:T(8,128)(2,1)S(1)} %copy-done.9), channel_id=1, source_target_pairs={{0,24},{8,0},{16,8},{24,16},{1,25},{9,1},{17,9},{25,17},{2,26},{10... | collective-permute-start | bytes 3145736 | tf_op jit(solution)/shard_map/ppermute | solution.py:433
  289.9 60.3 %collective-permute-start.23 = (bf16[256,2048]{1,0:T(8,128)(2,1)}, bf16[256,2048]{1,0:T(8,128)(2,1)}, u32[]{:S(2)}, u32[]{:S(2)}) collective-permute-start(bf16[256,2048]{1,0:T(8,128)(2,1)} %collective-permute-done.14.x_ref), channel_id=1, source_target_pairs={{0,24},{8,0},{16,8},{24,16},{1,25},{9,1},{17,9},{25,17},{2,26},{10... | collective-permute-start | bytes 3145736 | tf_op jit(solution)/shard_map/ppermute | solution.py:433
  314.9 86.5 %collective-permute-start.22 = (bf16[256,2048]{1,0:T(8,128)(2,1)}, bf16[256,2048]{1,0:T(8,128)(2,1)}, u32[]{:S(2)}, u32[]{:S(2)}) collective-permute-start(bf16[256,2048]{1,0:T(8,128)(2,1)} %collective-permute-done.21.x_ref), channel_id=1, source_target_pairs={{0,24},{8,0},{16,8},{24,16},{1,25},{9,1},{17,9},{25,17},{2,26},{10... | collective-permute-start | bytes 3145736 | tf_op jit(solution)/shard_map/ppermute | solution.py:433
  332.3 83.2 %collective-permute-start.26 = (bf16[256,2048]{1,0:T(8,128)(2,1)}, bf16[256,2048]{1,0:T(8,128)(2,1)S(1)}, u32[]{:S(2)}, u32[]{:S(2)}) collective-permute-start(bf16[256,2048]{1,0:T(8,128)(2,1)} %collective-permute-done.25.x_ref), channel_id=1, source_target_pairs={{0,24},{8,0},{16,8},{24,16},{1,25},{9,1},{17,9},{25,17},{2,26},{10... | collective-permute-start | bytes 3145736 | tf_op jit(solution)/shard_map/ppermute | solution.py:433
  350.2 84.2 %collective-permute-start.27 = (bf16[256,2048]{1,0:T(8,128)(2,1)}, bf16[256,2048]{1,0:T(8,128)(2,1)S(1)}, u32[]{:S(2)}, u32[]{:S(2)}) collective-permute-start(bf16[256,2048]{1,0:T(8,128)(2,1)} %collective-permute-done.24.x_ref), channel_id=1, source_target_pairs={{0,24},{8,0},{16,8},{24,16},{1,25},{9,1},{17,9},{25,17},{2,26},{10... | collective-permute-start | bytes 3145736 | tf_op jit(solution)/shard_map/ppermute | solution.py:433
  359.2 94.4 %collective-permute-start.28 = (bf16[256,2048]{1,0:T(8,128)(2,1)}, bf16[256,2048]{1,0:T(8,128)(2,1)S(1)}, u32[]{:S(2)}, u32[]{:S(2)}) collective-permute-start(bf16[256,2048]{1,0:T(8,128)(2,1)} %collective-permute-done.23.x_ref), channel_id=1, source_target_pairs={{0,24},{8,0},{16,8},{24,16},{1,25},{9,1},{17,9},{25,17},{2,26},{10... | collective-permute-start | bytes 3145736 | tf_op jit(solution)/shard_map/ppermute | solution.py:433
  (19 other events, 619.5 us)

commit v2 on v1

--- a/solution.py
+++ b/solution.py
@@ -196,7 +196,7 @@
             acc_ref[:, r] = jnp.zeros((acc_ref.shape[0], block), F32)
         for u in range(units):
 
-            @pl.when(which_ref[2 * units + u] != 0)
+            @pl.when(which_ref[2 * units + u * (count // block) + i] != 0)
             def _():
                 total = acc_ref[:, r]
                 for j in range(per):
@@ -245,7 +245,7 @@
     keys = refs[:hist]
     values = refs[hist : 2 * hist]
     x_hbm, w_hbm, acc_hbm = refs[2 * hist : 2 * hist + 3]
-    out_ref, k_ref, v_ref, x_ref, w_ref, acc_ref, xn, bias, sems = refs[2 * hist + 3 + aliased :]
+    out_ref, k_ref, v_ref, x_ref, w_ref, acc_ref, xn, bias, kall, vall, sems = refs[2 * hist + 3 + aliased :]
     rows, width = x_ref.shape
     f2 = width // per
     half = DH // 2
@@ -289,6 +289,10 @@
         a, b = u[:half], u[half:]
         c, s = cos_ref[...], sin_ref[...]
         return jnp.concatenate([a * c - b * s, b * c + a * s], axis=0)
+
+    for p in range(hist):
+        kall[:, edges[p] : edges[p + 1], :] = keys[p][...]
+        vall[:, :, edges[p] : edges[p + 1]] = values[p][...]
 
     def project(at):
         total = acc_ref[at, :]
@@ -305,31 +309,31 @@
         total = project(pl.ds(pl.multiple_of(base + (blocks - 1) * PAIR, PAIR), PAIR))
         k_ref[g] = rotary(total[:DH]).T.astype(BF16)
         v_ref[g] = total[DH:].astype(BF16)
-
+        kall[g, before:, :] = k_ref[g]
+        vall[g, :, before:] = v_ref[g]
+
+        def pair(i):
+            return project(pl.ds(pl.multiple_of(base + i * PAIR, PAIR), PAIR))
+
+        def score(total, h):
+            q = rotary(total[h * DH : (h + 1) * DH]).astype(BF16)
+            s = dot(kall[g], q, NN) * (math.log2(math.e) / math.sqrt(DH))
+            return s + bias[...]
+
+        def attend(scores, i, h):
+            expo = jnp.exp2(scores - scores.max(axis=0, keepdims=True))
+            scale = 1.0 / expo.sum(axis=0, keepdims=True)
+            out = dot(vall[g], expo.astype(BF16), NN)
+            at = pl.multiple_of((g * (blocks - 1) + i) * PAIR + h * DH, DH)
+            out_ref[:, pl.ds(at, DH)] = (out * scale).T.astype(BF16)
+
+        total = pair(0)
         for i in range(blocks - 1):
-            total = project(pl.ds(pl.multiple_of(base + i * PAIR, PAIR), PAIR))
+            scores = [score(total, h) for h in range(2)]
+            if i + 1 < blocks - 1:
+                total = pair(i + 1)
             for h in range(2):
-                q = rotary(total[h * DH : (h + 1) * DH]).astype(BF16)
-                scores = []
-                for p in range(hist + 1):
-                    src = keys[p] if p < hist else k_ref
-                    s = dot(src[g], q, NN) * (math.log2(math.e) / math.sqrt(DH))
-                    scores.append(s + bias[edges[p] : edges[p + 1], :])
-                top = scores[0].max(axis=0, keepdims=True)
-                for s in scores[1:]:
-                    top = jnp.maximum(top, s.max(axis=0, keepdims=True))
-                expo = [jnp.exp2(s - top) for s in scores]
-                norm = expo[0].sum(axis=0, keepdims=True)
-                for e in expo[1:]:
-                    norm = norm + e.sum(axis=0, keepdims=True)
-                scale = 1.0 / norm
-                out = None
-                for p in range(hist + 1):
-                    src = values[p] if p < hist else v_ref
-                    part = dot(src[g], expo[p].astype(BF16), NN)
-                    out = part if out is None else out + part
-                at = pl.multiple_of((g * (blocks - 1) + i) * PAIR + h * DH, DH)
-                out_ref[:, pl.ds(at, DH)] = (out * scale).T.astype(BF16)
+                attend(scores[h], i, h)
 
 
 def late(start, which, x, inv, gains, whole, per, acc, cos, sin, begin, past, out):
@@ -367,6 +371,8 @@
             pltpu.VMEM((cols, rows), F32),
             pltpu.VMEM((rows, width), BF16),
             pltpu.VMEM((wide, rows), F32),
+            pltpu.VMEM((groups, wide, DH), BF16),
+            pltpu.VMEM((groups, DH, wide), BF16),
             pltpu.SemaphoreType.DMA((1 + groups + groups * per,)),
         ],
     )
@@ -465,14 +471,19 @@
     far = (me ^ (pp - 2)) // per
     step_far = (far - z) % tp
     half_steps = tp // 2
+    blocks = count // min(count, 512)
+    block = jnp.arange(blocks, dtype=jnp.int32)[None, :]
     near = jnp.arange(half_steps, dtype=jnp.int32)
-    units1 = jnp.concatenate([near, which[:half_steps], near != step_far]).astype(jnp.int32)
-    late_steps = jnp.arange(half_steps, tp - 1, dtype=jnp.int32)
+    is_far = near == step_far
+    steps1 = jnp.where(is_far, half_steps, near)
+    flags1 = ~is_far[:, None] | (block < blocks // 2)
+    rest_steps = jnp.arange(half_steps, tp - 1, dtype=jnp.int32)
     waits = step_far < half_steps
-    early_far = jnp.where(waits, step_far, 0)[None]
-    units2 = jnp.concatenate(
-        [early_far, late_steps, (z + early_far) % tp, which[half_steps : tp - 1], waits[None], late_steps >= 0]
-    ).astype(jnp.int32)
+    steps2 = jnp.concatenate([jnp.where(waits, step_far, 0)[None], rest_steps])
+    flags2 = ~waits | (rest_steps != half_steps)[:, None] | (block >= blocks // 2)
+    flags2 = jnp.concatenate([jnp.broadcast_to(waits, (1, blocks)), flags2])
+    units1 = jnp.concatenate([steps1, (z + steps1) % tp, flags1.reshape(-1)]).astype(jnp.int32)
+    units2 = jnp.concatenate([steps2, (z + steps2) % tp, flags2.reshape(-1)]).astype(jnp.int32)
 
     seg = segment_ids[0]
     begin = jnp.sum((seg[None, :] < seg[:, None]).astype(jnp.int32), axis=1)
@@ -501,8 +512,8 @@
         where = jnp.concatenate([me[None], me ^ jnp.array(masks, jnp.int32)]).astype(jnp.int32)
         if n == len(stages) - 2:
             xs = prep(0, 0, tokens, inv, gains, None)
-            for k in range(1, half_steps):
-                for c in range(chunks):
+            for k in range(1, half_steps + 1):
+                for c in range(chunks if k < half_steps else chunks // 2):
                     xs = prep(k, c * rows, got[k - 1][c], inv, gains, xs)
             xs, cos, sin, inv, gains, units1, units2, which = lax.optimization_barrier(
                 (xs, cos, sin, inv, gains, units1, units2, which)
@@ -511,7 +522,7 @@
         state = place(state, where, items, groups * qrows, groups, pp)
     whole, weights_rows = state
     for k in range(half_steps, tp - 1):
-        for c in range(chunks):
+        for c in range(chunks // 2 if k == half_steps else 0, chunks):
             xs = prep(k, c * rows, got[k - 1][c], inv, gains, xs)
     acc = early(tp - half_steps, units2, xs, whole, per, acc)
 

time: 474 us -> 506 us (1.068)
  the two profiles are of different devices: /device:TPU:10 before, /device:TPU:0 now
where the time goes in v2:
time: 506 us; the launch traced here: 502 us
  waiting for transfers between devices  250 us (49%)
  Pallas kernels  190 us (38%)
  starting transfers between devices  39.1 us (8%)
  local copies, waits for them, and re-layouts  12.3 us (2%)
  other arithmetic  10.2 us (2%)
    ppermute x14, waiting for transfers between devices, swap(): return lax.ppermute(x, 'pp', [(i, i ^ mask) for i in range(pp)])  129 us
    ppermute x12, waiting for transfers between devices, layer(): step = [lax.ppermute(step[c], 'tp', ring) for c in range(chunks)]  77.9 us
    pallas_call x4, Pallas kernels, late(): pl.pallas_call(functools.partial(late_kernel, start, sizes, per, groups,...  57.3 us
    pallas_call x2, Pallas kernels, early(): pl.pallas_call(functools.partial(early_kernel, units, per, old), grid_spe...  56.9 us
    ppermute x3, waiting for transfers between devices, layer(): smalls.append(lax.ppermute(smalls[-1], 'tp', ring))  43.2 us
    pallas_call x5, Pallas kernels, place(): pl.pallas_call(functools.partial(place_kernel, pieces, old, groups, slice...  38.7 us
    pallas_call x9, Pallas kernels, prep(): pl.pallas_call(functools.partial(prep_kernel, k), grid=(rows // block,),...  28.3 us
    ppermute x12, starting transfers between devices, layer(): step = [lax.ppermute(step[c], 'tp', ring) for c in range(chunks)]  21.4 us
  transfers between devices with their start and end apart: 29, of which 10 were waited for; matrix products, arithmetic and copies ran while one was open for 3% of the time, Pallas kernels for 34%

profile of v2, /device:TPU:0, one launch (start us, length us, event | category | flops | bytes accessed | tf_op | source)
XLA Modules:
  0.0 502.3 jit_solution(14712698490690482874)
XLA Ops:
  18.2 40.4 %collective-permute-done.16 = f32[24,128]{1,0:T(8,128)S(1)} collective-permute-done((f32[24,128]{1,0:T(8,128)S(1)}, f32[24,128]{1,0:T(8,128)S(1)}, u32[]{:S(2)}, u32[]{:S(2)}) %collective-permute-start.16) | collective-permute-done | bytes 12320 | tf_op jit(solution)/shard_map/ppermute | solution.py:465
  58.6 4.3 collective-permute-start.17
  69.8 4.1 collective-permute-start.22
  74.0 23.4 %collective-permute-done.22.x_ref = bf16[256,2048]{1,0:T(8,128)(2,1)} collective-permute-done((bf16[256,2048]{1,0:T(8,128)(2,1)S(1)}, bf16[256,2048]{1,0:T(8,128)(2,1)}, u32[]{:S(2)}, u32[]{:S(2)}) %collective-permute-start.22) | collective-permute-done | bytes 1048608 | tf_op jit(solution)/shard_map/ppermute | solution.py:439
  97.4 4.4 collective-permute-start.15
  105.1 14.9 %collective-permute-done.21.x_ref = bf16[256,2048]{1,0:T(8,128)(2,1)} collective-permute-done((bf16[256,2048]{1,0:T(8,128)(2,1)}, bf16[256,2048]{1,0:T(8,128)(2,1)}, u32[]{:S(2)}, u32[]{:S(2)}) %collective-permute-start.21) | collective-permute-done | bytes 1048608 | tf_op jit(solution)/shard_map/ppermute | solution.py:439
  120.0 22.4 %collective-permute-done.20.x_ref = bf16[256,2048]{1,0:T(8,128)(2,1)} collective-permute-done((bf16[256,2048]{1,0:T(8,128)(2,1)S(1)}, bf16[256,2048]{1,0:T(8,128)(2,1)}, u32[]{:S(2)}, u32[]{:S(2)}) %collective-permute-start.20) | collective-permute-done | bytes 1048608 | tf_op jit(solution)/shard_map/ppermute | solution.py:439
  143.8 17.2 %collective-permute-done.15.x_ref = bf16[256,2048]{1,0:T(8,128)(2,1)} collective-permute-done((bf16[256,2048]{1,0:T(8,128)(2,1)}, bf16[256,2048]{1,0:T(8,128)(2,1)}, u32[]{:S(2)}, u32[]{:S(2)}) %collective-permute-start.15) | collective-permute-done | bytes 1048608 | tf_op jit(solution)/shard_map/ppermute | solution.py:439
  163.7 38.7 %collective-permute-done.3.refs_0_ = bf16[1280,1024]{1,0:T(8,128)(2,1)} collective-permute-done((bf16[1280,1024]{1,0:T(8,128)(2,1)}, bf16[1280,1024]{1,0:T(8,128)(2,1)}, u32[]{:S(2)}, u32[]{:S(2)}) %collective-permute-start.3) | collective-permute-done | bytes 2621472 | tf_op jit(solution)/shard_map/ppermute | solution.py:446
  203.0 55.6 %collective-permute-done.9.refs_0_ = bf16[1280,1024]{1,0:T(8,128)(2,1)} collective-permute-done((bf16[1280,1024]{1,0:T(8,128)(2,1)S(1)}, bf16[1280,1024]{1,0:T(8,128)(2,1)}, u32[]{:S(2)}, u32[]{:S(2)}) %collective-permute-start.9) | collective-permute-done | bytes 2621472 | tf_op jit(solution)/shard_map/ppermute | solution.py:446
  271.9 34.3 %collective-permute-done.1.refs_0_ = bf16[1280,1024]{1,0:T(8,128)(2,1)} collective-permute-done((bf16[1280,1024]{1,0:T(8,128)(2,1)}, bf16[1280,1024]{1,0:T(8,128)(2,1)}, u32[]{:S(2)}, u32[]{:S(2)}) %collective-permute-start.1) | collective-permute-done | bytes 2621472 | tf_op jit(solution)/shard_map/ppermute | solution.py:446
  307.3 5.8 %prep.9.refs_0_ = bf16[3,1024,2048]{2,1,0:T(8,128)(2,1)} custom-call(bf16[1024,2048]{1,0:T(8,128)(2,1)} %x_ref.1, f32[1024,1]{1,0:T(8,128)} %add_rsqrt_fusion.inv_ref, f32[4,2048]{1,0:T(4,128)} %pad_maximum_fusion.gain_ref), custom_call_target="tpu_custom_call" | custom-call | flops 209715200 | bytes 8388608 | tf_op jit(solution)/shard_map/prep/pallas_call | solution.py:148
  330.6 9.5 %place.5 = (bf16[8,2560,1024]{2,1,0:T(8,128)(2,1)}, bf16[2,160,8192]{2,1,0:T(8,128)(2,1)}) custom-call(s32[3]{0:T(128)} %pad_add_fusion.3.where_ref, bf16[1280,1024]{1,0:T(8,128)(2,1)} %cut.3.refs_0_, bf16[1280,1024]{1,0:T(8,128)(2,1)} %cut.4.refs_1_, bf16[1280,1024]{1,0:T(8,128)(2,1)} %collective-permute-done.12.refs_2_, ...), custom_call_target="tpu_custom_call" | custom-call | flops 1048576000 | bytes 20971520 | tf_op jit(solution)/shard_map/place/pallas_call | solution.py:120
  340.1 4.4 collective-permute-start.25
  344.6 9.5 %place.6 = (bf16[8,2560,1024]{2,1,0:T(8,128)(2,1)}, bf16[2,160,8192]{2,1,0:T(8,128)(2,1)}) custom-call(s32[5]{0:T(128)} %pad_add_fusion.2.where_ref, bf16[1280,1024]{1,0:T(8,128)(2,1)} %collective-permute-done.9.refs_0_, bf16[1280,1024]{1,0:T(8,128)(2,1)} %collective-permute-done.10.refs_1_, ...), custom_call_target="tpu_custom_call", output_to_operand_aliasing={{0}: (5, {}), {1}: (6, {})} | custom-call | flops 1048576000 | bytes 20971520 | tf_op jit(solution)/shard_map/place/pallas_call | solution.py:120
  355.6 9.5 %place.7 = (bf16[8,2560,1024]{2,1,0:T(8,128)(2,1)}, bf16[2,160,8192]{2,1,0:T(8,128)(2,1)}) custom-call(s32[5]{0:T(128)} %pad_add_fusion.2.where_ref, bf16[1280,1024]{1,0:T(8,128)(2,1)} %collective-permute-done.3.refs_0_, bf16[1280,1024]{1,0:T(8,128)(2,1)} %copy-done.2, ...), custom_call_target="tpu_custom_call", output_to_operand_aliasing={{0}: (5, {}), {1}: (6, {})} | custom-call | flops 1048576000 | bytes 20971520 | tf_op jit(solution)/shard_map/place/pallas_call | solution.py:120
  365.2 33.2 %early.2.refs_2_ = f32[2560,1024]{1,0:T(8,128)} custom-call(s32[8]{0:T(128)} %pad_add_fusion.4.which_ref, bf16[3,1024,2048]{2,1,0:T(8,128)(2,1)} %prep.15.refs_0_.x_hbm, bf16[4,2,2560,1024]{3,2,1,0:T(8,128)(2,1)} %bitcast.17, bf16[4,2,2560,1024]{3,2,1,0:T(8,128)(2,1)} %bitcast.18), custom_call_target="tpu_custom_call" | custom-call | flops 21474836480 | bytes 39845888 | tf_op jit(solution)/shard_map/early/pallas_call | solution.py:228
  404.1 5.0 %place.8 = (bf16[8,2560,1024]{2,1,0:T(8,128)(2,1)}, bf16[2,160,8192]{2,1,0:T(8,128)(2,1)}) custom-call(s32[2]{0:T(128)} %pad_add_fusion.1.where_ref, bf16[1280,1024]{1,0:T(8,128)(2,1)} %collective-permute-done.1.refs_0_, bf16[1280,1024]{1,0:T(8,128)(2,1)} %collective-permute-done.4.refs_1_, ...), custom_call_target="tpu_custom_call", output_to_operand_aliasing={{0}: (3, {}), {1}: (4, {})} | custom-call | flops 524288000 | bytes 10485760 | tf_op jit(solution)/shard_map/place/pallas_call | solution.py:120
  413.0 5.0 %place.9 = (bf16[8,2560,1024]{2,1,0:T(8,128)(2,1)}, bf16[2,160,8192]{2,1,0:T(8,128)(2,1)}) custom-call(s32[2]{0:T(128)} %pad_add_fusion.where_ref, bf16[1280,1024]{1,0:T(8,128)(2,1)} %collective-permute-done.2.refs_0_, bf16[1280,1024]{1,0:T(8,128)(2,1)} %collective-permute-done.5.refs_1_, ...), custom_call_target="tpu_custom_call", output_to_operand_aliasing={{0}: (3, {}), {1}: (4, {})} | custom-call | flops 524288000 | bytes 10485760 | tf_op jit(solution)/shard_map/place/pallas_call | solution.py:120
  418.0 23.6 %early.3.refs_2_.refs_4_.refs_6_ = f32[2560,1024]{1,0:T(8,128)} custom-call(s32[8]{0:T(128)} %pad_add_fusion.5.which_ref, bf16[3,1024,2048]{2,1,0:T(8,128)(2,1)} %prep.17.x_hbm, bf16[4,2,2560,1024]{3,2,1,0:T(8,128)(2,1)} %bitcast.19, bf16[4,2,2560,1024]{3,2,1,0:T(8,128)(2,1)} %bitcast.20, f32[2560,1024]{1,0:T(8,128)} %early.2.refs_2_), custom_call_target="tpu_custom_call", output_to_operand_aliasing={{}: (4, {})} | custom-call | flops 21474836480 | bytes 50331648 | tf_op jit(solution)/shard_map/early/pallas_call | solution.py:228
  441.7 13.4 %late.4 = (bf16[1024,2048]{1,0:T(8,128)(2,1)}, bf16[2,256,128]{2,1,0:T(8,128)(2,1)}, bf16[2,128,256]{2,1,0:T(8,128)(2,1)}) custom-call(s32[1]{0:T(128)} %slice.57.which_ref, f32[1024,1]{1,0:T(8,128)} %add_rsqrt_fusion.inv_ref, f32[4,2048]{1,0:T(4,128)} %pad_maximum_fusion.gain_ref, f32[64,1024]{1,0:T(8,128)} %get-tuple-element.46.cos_ref, ...), custom_call_target="tpu_custom_call" | custom-call | flops 3221225472 | bytes 14155776 | tf_op jit(solution)/shard_map/late/pallas_call | solution.py:379
  456.1 14.5 %late.5 = (bf16[1024,2048]{1,0:T(8,128)(2,1)}, bf16[2,256,128]{2,1,0:T(8,128)(2,1)}, bf16[2,128,256]{2,1,0:T(8,128)(2,1)}) custom-call(s32[1]{0:T(128)} %slice.57.which_ref, f32[1024,1]{1,0:T(8,128)} %add_rsqrt_fusion.inv_ref, f32[4,2048]{1,0:T(4,128)} %pad_maximum_fusion.gain_ref, ...), custom_call_target="tpu_custom_call", output_to_operand_aliasing={{0}: (11, {})} | custom-call | flops 3758096384 | bytes 14155776 | tf_op jit(solution)/shard_map/late/pallas_call | solution.py:379
  471.7 14.7 %late.6 = (bf16[1024,2048]{1,0:T(8,128)(2,1)}, bf16[2,256,128]{2,1,0:T(8,128)(2,1)}, bf16[2,128,256]{2,1,0:T(8,128)(2,1)}) custom-call(s32[1]{0:T(128)} %slice.57.which_ref, f32[1024,1]{1,0:T(8,128)} %add_rsqrt_fusion.inv_ref, f32[4,2048]{1,0:T(4,128)} %pad_maximum_fusion.gain_ref, ...), custom_call_target="tpu_custom_call", output_to_operand_aliasing={{0}: (13, {})} | custom-call | flops 4294967296 | bytes 14155776 | tf_op jit(solution)/shard_map/late/pallas_call | solution.py:379
  487.4 14.7 %late.7 = (bf16[1024,2048]{1,0:T(8,128)(2,1)}, bf16[2,256,128]{2,1,0:T(8,128)(2,1)}, bf16[2,128,256]{2,1,0:T(8,128)(2,1)}) custom-call(s32[1]{0:T(128)} %slice.57.which_ref, f32[1024,1]{1,0:T(8,128)} %add_rsqrt_fusion.inv_ref, f32[4,2048]{1,0:T(4,128)} %pad_maximum_fusion.gain_ref, ...), custom_call_target="tpu_custom_call", output_to_operand_aliasing={{0}: (13, {})} | custom-call | flops 4294967296 | bytes 14155776 | tf_op jit(solution)/shard_map/late/pallas_call | solution.py:379
  (117 shorter events, 78.5 us)
Async XLA Ops:
  3.9 158.7 %collective-permute-start.12 = (bf16[1280,1024]{1,0:T(8,128)(2,1)}, bf16[1280,1024]{1,0:T(8,128)(2,1)}, u32[]{:S(2)}, u32[]{:S(2)}) collective-permute-start(bf16[1280,1024]{1,0:T(8,128)(2,1)} %cut.3.refs_0_), channel_id=1, source_target_pairs={{0,1},{1,0},{2,3},{3,2},{4,5},{5,4},{6,7},{7,6},{8,9},{9,8},{10,11... | collective-permute-start | bytes 7864328 | tf_op jit(solution)/shard_map/ppermute | solution.py:446
  4.4 158.6 %collective-permute-start = (bf16[1280,1024]{1,0:T(8,128)(2,1)}, bf16[1280,1024]{1,0:T(8,128)(2,1)}, u32[]{:S(2)}, u32[]{:S(2)}) collective-permute-start(bf16[1280,1024]{1,0:T(8,128)(2,1)} %cut.3.refs_0_), channel_id=1, source_target_pairs={{0,4},{1,5},{2,6},{3,7},{4,0},{5,1},{6,2},{7,3},{8,12},{9,13},{10,... | collective-permute-start | bytes 7864328 | tf_op jit(solution)/shard_map/ppermute | solution.py:446
  9.3 64.6 %collective-permute-start.19 = (bf16[256,2048]{1,0:T(8,128)(2,1)}, bf16[256,2048]{1,0:T(8,128)(2,1)S(1)}, u32[]{:S(2)}, u32[]{:S(2)}) collective-permute-start(bf16[256,2048]{1,0:T(8,128)(2,1)} %cut.5), channel_id=1, source_target_pairs={{0,24},{8,0},{16,8},{24,16},{1,25},{9,1},{17,9},{25,17},{2,26},{10... | collective-permute-start | bytes 3145736 | tf_op jit(solution)/shard_map/ppermute | solution.py:439
  16.1 57.9 %collective-permute-start.14 = (bf16[256,2048]{1,0:T(8,128)(2,1)S(1)}, bf16[256,2048]{1,0:T(8,128)(2,1)}, u32[]{:S(2)}, u32[]{:S(2)}) collective-permute-start(bf16[256,2048]{1,0:T(8,128)(2,1)S(1)} %get-tuple-element.64), channel_id=1, source_target_pairs={{0,24},{8,0},{16,8},{24,16},{1,25},{9,1},{17,9},{25,17},{2,26},{10... | collective-permute-start | bytes 3145736 | tf_op jit(solution)/shard_map/ppermute | solution.py:439
  73.9 46.1 %collective-permute-start.21 = (bf16[256,2048]{1,0:T(8,128)(2,1)}, bf16[256,2048]{1,0:T(8,128)(2,1)}, u32[]{:S(2)}, u32[]{:S(2)}) collective-permute-start(bf16[256,2048]{1,0:T(8,128)(2,1)} %get-tuple-element.63), channel_id=1, source_target_pairs={{0,24},{8,0},{16,8},{24,16},{1,25},{9,1},{17,9},{25,17},{2,26},{10... | collective-permute-start | bytes 3145736 | tf_op jit(solution)/shard_map/ppermute | solution.py:439
  73.9 68.4 %collective-permute-start.20 = (bf16[256,2048]{1,0:T(8,128)(2,1)S(1)}, bf16[256,2048]{1,0:T(8,128)(2,1)}, u32[]{:S(2)}, u32[]{:S(2)}) collective-permute-start(bf16[256,2048]{1,0:T(8,128)(2,1)S(1)} %collective-permute-done.19.x_ref), channel_id=1, source_target_pairs={{0,24},{8,0},{16,8},{24,16},{1,25},{9,1},{17,9},{25,17},{2,26},{10... | collective-permute-start | bytes 3145736 | tf_op jit(solution)/shard_map/ppermute | solution.py:439
  97.4 63.6 %collective-permute-start.15 = (bf16[256,2048]{1,0:T(8,128)(2,1)}, bf16[256,2048]{1,0:T(8,128)(2,1)}, u32[]{:S(2)}, u32[]{:S(2)}) collective-permute-start(bf16[256,2048]{1,0:T(8,128)(2,1)} %collective-permute-done.14.x_ref), channel_id=1, source_target_pairs={{0,24},{8,0},{16,8},{24,16},{1,25},{9,1},{17,9},{25,17},{2,26},{10... | collective-permute-start | bytes 3145736 | tf_op jit(solution)/shard_map/ppermute | solution.py:439
  142.3 60.1 %collective-permute-start.3 = (bf16[1280,1024]{1,0:T(8,128)(2,1)}, bf16[1280,1024]{1,0:T(8,128)(2,1)}, u32[]{:S(2)}, u32[]{:S(2)}) collective-permute-start(bf16[1280,1024]{1,0:T(8,128)(2,1)} %cut.4.refs_1_), channel_id=1, source_target_pairs={{0,2},{1,3},{2,0},{3,1},{4,6},{5,7},{6,4},{7,5},{8,10},{9,11},{10,... | collective-permute-start | bytes 7864328 | tf_op jit(solution)/shard_map/ppermute | solution.py:446
  161.1 97.5 %collective-permute-start.9 = (bf16[1280,1024]{1,0:T(8,128)(2,1)S(1)}, bf16[1280,1024]{1,0:T(8,128)(2,1)}, u32[]{:S(2)}, u32[]{:S(2)}) collective-permute-start(bf16[1280,1024]{1,0:T(8,128)(2,1)S(1)} %copy-done.1), channel_id=1, source_target_pairs={{0,2},{1,3},{2,0},{3,1},{4,6},{5,7},{6,4},{7,5},{8,10},{9,11},{10,... | collective-permute-start | bytes 7864328 | tf_op jit(solution)/shard_map/ppermute | solution.py:446
  162.6 96.0 %collective-permute-start.7 = (bf16[1280,1024]{1,0:T(8,128)(2,1)}, bf16[1280,1024]{1,0:T(8,128)(2,1)}, u32[]{:S(2)}, u32[]{:S(2)}) collective-permute-start(bf16[1280,1024]{1,0:T(8,128)(2,1)} %cut.4.refs_1_), channel_id=1, source_target_pairs={{0,4},{1,5},{2,6},{3,7},{4,0},{5,1},{6,2},{7,3},{8,12},{9,13},{10,... | collective-permute-start | bytes 7864328 | tf_op jit(solution)/shard_map/ppermute | solution.py:446
  163.1 96.0 %collective-permute-start.11 = (bf16[1280,1024]{1,0:T(8,128)(2,1)}, bf16[1280,1024]{1,0:T(8,128)(2,1)}, u32[]{:S(2)}, u32[]{:S(2)}) collective-permute-start(bf16[1280,1024]{1,0:T(8,128)(2,1)} %collective-permute-done.refs_2_), channel_id=1, source_target_pairs={{0,1},{1,0},{2,3},{3,2},{4,5},{5,4},{6,7},{7,6},{8,9},{9,8},{10,11... | collective-permute-start | bytes 7864328 | tf_op jit(solution)/shard_map/ppermute | solution.py:446
  163.1 143.1 %collective-permute-start.1 = (bf16[1280,1024]{1,0:T(8,128)(2,1)}, bf16[1280,1024]{1,0:T(8,128)(2,1)}, u32[]{:S(2)}, u32[]{:S(2)}) collective-permute-start(bf16[1280,1024]{1,0:T(8,128)(2,1)} %collective-permute-done.refs_2_), channel_id=1, source_target_pairs={{0,2},{1,3},{2,0},{3,1},{4,6},{5,7},{6,4},{7,5},{8,10},{9,11},{10,... | collective-permute-start | bytes 7864328 | tf_op jit(solution)/shard_map/ppermute | solution.py:446
  202.4 103.8 %collective-permute-start.4 = (bf16[1280,1024]{1,0:T(8,128)(2,1)}, bf16[1280,1024]{1,0:T(8,128)(2,1)}, u32[]{:S(2)}, u32[]{:S(2)}) collective-permute-start(bf16[1280,1024]{1,0:T(8,128)(2,1)} %collective-permute-done.3.refs_0_), channel_id=1, source_target_pairs={{0,4},{1,5},{2,6},{3,7},{4,0},{5,1},{6,2},{7,3},{8,12},{9,13},{10,... | collective-permute-start | bytes 7864328 | tf_op jit(solution)/shard_map/ppermute | solution.py:446
  258.6 95.6 %collective-permute-start.6 = (bf16[1280,1024]{1,0:T(8,128)(2,1)}, bf16[1280,1024]{1,0:T(8,128)(2,1)S(1)}, u32[]{:S(2)}, u32[]{:S(2)}) collective-permute-start(bf16[1280,1024]{1,0:T(8,128)(2,1)} %collective-permute-done.3.refs_0_), channel_id=1, source_target_pairs={{0,1},{1,0},{2,3},{3,2},{4,5},{5,4},{6,7},{7,6},{8,9},{9,8},{10,11... | collective-permute-start | bytes 7864328 | tf_op jit(solution)/shard_map/ppermute | solution.py:446
  258.6 81.6 %collective-permute-start.10 = (bf16[1280,1024]{1,0:T(8,128)(2,1)}, bf16[1280,1024]{1,0:T(8,128)(2,1)}, u32[]{:S(2)}, u32[]{:S(2)}) collective-permute-start(bf16[1280,1024]{1,0:T(8,128)(2,1)} %collective-permute-done.9.refs_0_), channel_id=1, source_target_pairs={{0,1},{1,0},{2,3},{3,2},{4,5},{5,4},{6,7},{7,6},{8,9},{9,8},{10,11... | collective-permute-start | bytes 7864328 | tf_op jit(solution)/shard_map/ppermute | solution.py:446
  259.1 95.1 %collective-permute-start.8 = (bf16[1280,1024]{1,0:T(8,128)(2,1)}, bf16[1280,1024]{1,0:T(8,128)(2,1)}, u32[]{:S(2)}, u32[]{:S(2)}) collective-permute-start(bf16[1280,1024]{1,0:T(8,128)(2,1)} %collective-permute-done.7.refs_2_), channel_id=1, source_target_pairs={{0,1},{1,0},{2,3},{3,2},{4,5},{5,4},{6,7},{7,6},{8,9},{9,8},{10,11... | collective-permute-start | bytes 7864328 | tf_op jit(solution)/shard_map/ppermute | solution.py:446
  306.2 103.0 %collective-permute-start.2 = (bf16[1280,1024]{1,0:T(8,128)(2,1)}, bf16[1280,1024]{1,0:T(8,128)(2,1)}, u32[]{:S(2)}, u32[]{:S(2)}) collective-permute-start(bf16[1280,1024]{1,0:T(8,128)(2,1)} %collective-permute-done.1.refs_0_), channel_id=1, source_target_pairs={{0,1},{1,0},{2,3},{3,2},{4,5},{5,4},{6,7},{7,6},{8,9},{9,8},{10,11... | collective-permute-start | bytes 7864328 | tf_op jit(solution)/shard_map/ppermute | solution.py:446
  306.2 106.8 %collective-permute-start.5 = (bf16[1280,1024]{1,0:T(8,128)(2,1)}, bf16[1280,1024]{1,0:T(8,128)(2,1)}, u32[]{:S(2)}, u32[]{:S(2)}) collective-permute-start(bf16[1280,1024]{1,0:T(8,128)(2,1)} %collective-permute-done.4.refs_1_), channel_id=1, source_target_pairs={{0,1},{1,0},{2,3},{3,2},{4,5},{5,4},{6,7},{7,6},{8,9},{9,8},{10,11... | collective-permute-start | bytes 7864328 | tf_op jit(solution)/shard_map/ppermute | solution.py:446
  340.1 58.3 %collective-permute-start.25 = (bf16[256,2048]{1,0:T(8,128)(2,1)}, bf16[256,2048]{1,0:T(8,128)(2,1)}, u32[]{:S(2)}, u32[]{:S(2)}) collective-permute-start(bf16[256,2048]{1,0:T(8,128)(2,1)} %collective-permute-done.22.x_ref), channel_id=1, source_target_pairs={{0,24},{8,0},{16,8},{24,16},{1,25},{9,1},{17,9},{25,17},{2,26},{10... | collective-permute-start | bytes 3145736 | tf_op jit(solution)/shard_map/ppermute | solution.py:439
  354.2 47.2 %collective-permute-start.24 = (bf16[256,2048]{1,0:T(8,128)(2,1)}, bf16[256,2048]{1,0:T(8,128)(2,1)}, u32[]{:S(2)}, u32[]{:S(2)}) collective-permute-start(bf16[256,2048]{1,0:T(8,128)(2,1)} %collective-permute-done.21.x_ref), channel_id=1, source_target_pairs={{0,24},{8,0},{16,8},{24,16},{1,25},{9,1},{17,9},{25,17},{2,26},{10... | collective-permute-start | bytes 3145736 | tf_op jit(solution)/shard_map/ppermute | solution.py:439
  354.2 87.4 %collective-permute-start.23 = (bf16[256,2048]{1,0:T(8,128)(2,1)}, bf16[256,2048]{1,0:T(8,128)(2,1)}, u32[]{:S(2)}, u32[]{:S(2)}) collective-permute-start(bf16[256,2048]{1,0:T(8,128)(2,1)} %collective-permute-done.20.x_ref), channel_id=1, source_target_pairs={{0,24},{8,0},{16,8},{24,16},{1,25},{9,1},{17,9},{25,17},{2,26},{10... | collective-permute-start | bytes 3145736 | tf_op jit(solution)/shard_map/ppermute | solution.py:439
  398.5 56.6 %collective-permute-start.26 = (bf16[256,2048]{1,0:T(8,128)(2,1)}, bf16[256,2048]{1,0:T(8,128)(2,1)S(1)}, u32[]{:S(2)}, u32[]{:S(2)}) collective-permute-start(bf16[256,2048]{1,0:T(8,128)(2,1)} %collective-permute-done.15.x_ref), channel_id=1, source_target_pairs={{0,24},{8,0},{16,8},{24,16},{1,25},{9,1},{17,9},{25,17},{2,26},{10... | collective-permute-start | bytes 3145736 | tf_op jit(solution)/shard_map/ppermute | solution.py:439
  401.3 69.3 %collective-permute-start.27 = (bf16[256,2048]{1,0:T(8,128)(2,1)}, bf16[256,2048]{1,0:T(8,128)(2,1)S(1)}, u32[]{:S(2)}, u32[]{:S(2)}) collective-permute-start(bf16[256,2048]{1,0:T(8,128)(2,1)} %collective-permute-done.25.x_ref), channel_id=1, source_target_pairs={{0,24},{8,0},{16,8},{24,16},{1,25},{9,1},{17,9},{25,17},{2,26},{10... | collective-permute-start | bytes 3145736 | tf_op jit(solution)/shard_map/ppermute | solution.py:439
  409.2 77.2 %collective-permute-start.28 = (bf16[256,2048]{1,0:T(8,128)(2,1)}, bf16[256,2048]{1,0:T(8,128)(2,1)S(1)}, u32[]{:S(2)}, u32[]{:S(2)}) collective-permute-start(bf16[256,2048]{1,0:T(8,128)(2,1)} %collective-permute-done.24.x_ref), channel_id=1, source_target_pairs={{0,24},{8,0},{16,8},{24,16},{1,25},{9,1},{17,9},{25,17},{2,26},{10... | collective-permute-start | bytes 3145736 | tf_op jit(solution)/shard_map/ppermute | solution.py:439
  (16 other events, 751.2 us)

commit v3 on v2

--- a/solution.py
+++ b/solution.py
@@ -28,7 +28,7 @@
     return lax.dot_general(a, b, dims, preferred_element_type=F32)
 
 
-def params(mib=56):
+def params(mib=63):
     return pltpu.CompilerParams(vmem_limit_bytes=mib << 20)
 
 
@@ -47,7 +47,7 @@
         put(start + r, step, y.astype(BF16))
 
 
-def place_kernel(pieces, old, groups, slices, where_ref, *refs):
+def place_kernel(pieces, cuts, old, groups, slices, where_ref, *refs):
     count = len(pieces)
     ins = refs[:count]
     out, rows_out, buf, sem_in, sem_out, sem_rows = refs[count + 2 * old :]
@@ -60,13 +60,16 @@
         spots.append(pl.ds(used, size))
         used += size
 
-    def get(i):
-        return pltpu.make_async_copy(ins[i], buf.at[spots[i]], sem_in.at[i])
-
-    def put(i):
+    def get(i, t):
+        size = pieces[i][2] // cuts
+        src = ins[i].at[pl.ds(t * size, size), :]
+        return pltpu.make_async_copy(src, buf.at[pl.ds(spots[i].start + t * size, size)], sem_in.at[i, t])
+
+    def put(i, t):
         which, first, size = pieces[i]
-        at = out.at[where_ref[1 + which], pl.ds(first, size), :]
-        return pltpu.make_async_copy(buf.at[spots[i]], at, sem_out.at[i])
+        size = size // cuts
+        at = out.at[where_ref[1 + which], pl.ds(first + t * size, size), :]
+        return pltpu.make_async_copy(buf.at[pl.ds(spots[i].start + t * size, size)], at, sem_out.at[i, t])
 
     def each(i, act):
         which, first, size = pieces[i]
@@ -87,19 +90,23 @@
                 pl.when((at >= 0) & (at < size))(go)
 
     for i in range(count):
-        get(i).start()
+        for t in range(cuts):
+            get(i, t).start()
     for i in range(count):
-        get(i).wait()
-        put(i).start()
+        for t in range(cuts):
+            get(i, t).wait()
+            put(i, t).start()
         each(i, lambda copy: copy.start())
     for i in range(count):
-        put(i).wait()
+        for t in range(cuts):
+            put(i, t).wait()
         each(i, lambda copy: copy.wait())
 
 
 def place(state, where, items, rows, groups, slices):
     arrays = [x for _, _, x in items]
     pieces = [(which, first, x.shape[0]) for which, first, x in items]
+    cuts = 4 if len(items) <= 4 else 2
     width = arrays[0].shape[1]
     count = len(arrays)
     total = sum(size for _, _, size in pieces)
@@ -111,14 +118,14 @@
         out_specs=[any_spec()] * 2,
         scratch_shapes=[
             pltpu.VMEM((total, width), BF16),
-            pltpu.SemaphoreType.DMA((count,)),
-            pltpu.SemaphoreType.DMA((count,)),
+            pltpu.SemaphoreType.DMA((count, cuts)),
+            pltpu.SemaphoreType.DMA((count, cuts)),
             pltpu.SemaphoreType.DMA((count, groups)),
         ],
     )
     size = total * width * 2
     return pl.pallas_call(
-        functools.partial(place_kernel, pieces, old, groups, slices),
+        functools.partial(place_kernel, pieces, cuts, old, groups, slices),
         grid_spec=grid,
         out_shape=(
             jax.ShapeDtypeStruct((slices, rows, width), BF16),
@@ -142,7 +149,7 @@
 
 def prep(k, start, x, inv, gains, out):
     rows, width = x.shape
-    block = min(rows, 256)
+    block = min(rows, 128)
     at = start // block
     extra = 0 if out is None else 1
     return pl.pallas_call(
@@ -230,7 +237,7 @@
         grid_spec=grid,
         out_shape=jax.ShapeDtypeStruct((rows, count), F32),
         input_output_aliases={2 + units: 0} if old else {},
-        compiler_params=params(60),
+        compiler_params=params(),
         cost_estimate=pl.CostEstimate(
             flops=2 * count * width * units * rows,
             bytes_accessed=units * width * (rows + count) * 2 + count * rows * 4 * (1 + old),
@@ -398,20 +405,39 @@
     )
 
 
-def cut_kernel(first, size, x_hbm, o_ref, sem):
-    copy = pltpu.make_async_copy(x_hbm.at[pl.ds(first, size)], o_ref, sem)
-    copy.start()
-    copy.wait()
+def cut_kernel(first, size, cuts, x_hbm, o_hbm, buf, sem_in, sem_out):
+    step = size // cuts
+
+    def get(t):
+        at = pl.ds(t * step, step)
+        return pltpu.make_async_copy(x_hbm.at[pl.ds(first + t * step, step)], buf.at[at], sem_in.at[t])
+
+    def put(t):
+        at = pl.ds(t * step, step)
+        return pltpu.make_async_copy(buf.at[at], o_hbm.at[at], sem_out.at[t])
+
+    for t in range(cuts):
+        get(t).start()
+    for t in range(cuts):
+        get(t).wait()
+        put(t).start()
+    for t in range(cuts):
+        put(t).wait()
 
 
 def cut(x, first, size):
+    cuts = 4
     return pl.pallas_call(
-        functools.partial(cut_kernel, first, size),
+        functools.partial(cut_kernel, first, size, cuts),
         in_specs=[any_spec()],
-        out_specs=pl.BlockSpec(memory_space=pltpu.VMEM),
+        out_specs=any_spec(),
         out_shape=jax.ShapeDtypeStruct((size, x.shape[1]), x.dtype),
-        scratch_shapes=[pltpu.SemaphoreType.DMA],
-        compiler_params=params(60),
+        scratch_shapes=[
+            pltpu.VMEM((size, x.shape[1]), x.dtype),
+            pltpu.SemaphoreType.DMA((cuts,)),
+            pltpu.SemaphoreType.DMA((cuts,)),
+        ],
+        compiler_params=params(),
         name="cut",
     )(x)
 

time: 506 us -> 500 us (0.988)
  local copies, waits for them, and re-layouts: 12.3 us -> 4.78 us
where the time goes in v3:
time: 500 us; the launch traced here: 496 us
  waiting for transfers between devices  255 us (51%)
  Pallas kernels  187 us (37%)
  starting transfers between devices  40.3 us (8%)
  other arithmetic  8.7 us (2%)
    ppermute x14, waiting for transfers between devices, swap(): return lax.ppermute(x, 'pp', [(i, i ^ mask) for i in range(pp)])  133 us
    ppermute x12, waiting for transfers between devices, layer(): step = [lax.ppermute(step[c], 'tp', ring) for c in range(chunks)]  78.5 us
    pallas_call x4, Pallas kernels, late(): pl.pallas_call(functools.partial(late_kernel, start, sizes, per, groups,...  57 us
    pallas_call x2, Pallas kernels, early(): pl.pallas_call(functools.partial(early_kernel, units, per, old), grid_spe...  56.8 us
    ppermute x3, waiting for transfers between devices, layer(): smalls.append(lax.ppermute(smalls[-1], 'tp', ring))  43.2 us
    pallas_call x5, Pallas kernels, place(): pl.pallas_call(functools.partial(place_kernel, pieces, cuts, old, groups,...  38.7 us
    pallas_call x9, Pallas kernels, prep(): pl.pallas_call(functools.partial(prep_kernel, k), grid=(rows // block,),...  26.8 us
    ppermute x12, starting transfers between devices, layer(): step = [lax.ppermute(step[c], 'tp', ring) for c in range(chunks)]  22.6 us
  transfers between devices with their start and end apart: 29, of which 10 were waited for; matrix products, arithmetic and copies ran while one was open for 3% of the time, Pallas kernels for 34%

profile of v3, /device:TPU:0, one launch (start us, length us, event | category | flops | bytes accessed | tf_op | source)
XLA Modules:
  0.0 496.4 jit_solution(12814358834122522837)
XLA Ops:
  17.4 40.4 %collective-permute-done.16 = f32[24,128]{1,0:T(8,128)S(1)} collective-permute-done((f32[24,128]{1,0:T(8,128)S(1)}, f32[24,128]{1,0:T(8,128)S(1)}, u32[]{:S(2)}, u32[]{:S(2)}) %collective-permute-start.16) | collective-permute-done | bytes 12320 | tf_op jit(solution)/shard_map/ppermute | solution.py:491
  57.8 4.3 collective-permute-start.17
  73.2 23.4 %collective-permute-done.22.x_ref = bf16[256,2048]{1,0:T(8,128)(2,1)} collective-permute-done((bf16[256,2048]{1,0:T(8,128)(2,1)S(1)}, bf16[256,2048]{1,0:T(8,128)(2,1)}, u32[]{:S(2)}, u32[]{:S(2)}) %collective-permute-start.22) | collective-permute-done | bytes 1048608 | tf_op jit(solution)/shard_map/ppermute | solution.py:465
  96.6 4.4 collective-permute-start.15
  103.7 15.5 %collective-permute-done.21.x_ref = bf16[256,2048]{1,0:T(8,128)(2,1)} collective-permute-done((bf16[256,2048]{1,0:T(8,128)(2,1)}, bf16[256,2048]{1,0:T(8,128)(2,1)}, u32[]{:S(2)}, u32[]{:S(2)}) %collective-permute-start.21) | collective-permute-done | bytes 1048608 | tf_op jit(solution)/shard_map/ppermute | solution.py:465
  119.2 22.5 %collective-permute-done.20.x_ref = bf16[256,2048]{1,0:T(8,128)(2,1)} collective-permute-done((bf16[256,2048]{1,0:T(8,128)(2,1)}, bf16[256,2048]{1,0:T(8,128)(2,1)}, u32[]{:S(2)}, u32[]{:S(2)}) %collective-permute-start.20) | collective-permute-done | bytes 1048608 | tf_op jit(solution)/shard_map/ppermute | solution.py:465
  143.1 17.1 %collective-permute-done.15.x_ref = bf16[256,2048]{1,0:T(8,128)(2,1)} collective-permute-done((bf16[256,2048]{1,0:T(8,128)(2,1)}, bf16[256,2048]{1,0:T(8,128)(2,1)}, u32[]{:S(2)}, u32[]{:S(2)}) %collective-permute-start.15) | collective-permute-done | bytes 1048608 | tf_op jit(solution)/shard_map/ppermute | solution.py:465
  162.9 38.8 %collective-permute-done.3.refs_0_ = bf16[1280,1024]{1,0:T(8,128)(2,1)} collective-permute-done((bf16[1280,1024]{1,0:T(8,128)(2,1)}, bf16[1280,1024]{1,0:T(8,128)(2,1)}, u32[]{:S(2)}, u32[]{:S(2)}) %collective-permute-start.3) | collective-permute-done | bytes 2621472 | tf_op jit(solution)/shard_map/ppermute | solution.py:472
  202.3 55.6 %collective-permute-done.9.refs_0_ = bf16[1280,1024]{1,0:T(8,128)(2,1)} collective-permute-done((bf16[1280,1024]{1,0:T(8,128)(2,1)}, bf16[1280,1024]{1,0:T(8,128)(2,1)}, u32[]{:S(2)}, u32[]{:S(2)}) %collective-permute-start.9) | collective-permute-done | bytes 2621472 | tf_op jit(solution)/shard_map/ppermute | solution.py:472
  266.7 38.8 %collective-permute-done.1.refs_0_ = bf16[1280,1024]{1,0:T(8,128)(2,1)} collective-permute-done((bf16[1280,1024]{1,0:T(8,128)(2,1)}, bf16[1280,1024]{1,0:T(8,128)(2,1)}, u32[]{:S(2)}, u32[]{:S(2)}) %collective-permute-start.1) | collective-permute-done | bytes 2621472 | tf_op jit(solution)/shard_map/ppermute | solution.py:472
  306.6 7.5 %prep.9.refs_0_ = bf16[3,1024,2048]{2,1,0:T(8,128)(2,1)} custom-call(bf16[1024,2048]{1,0:T(8,128)(2,1)} %x_ref.1, f32[1024,1]{1,0:T(8,128)} %add_rsqrt_fusion.inv_ref, f32[4,2048]{1,0:T(4,128)} %pad_maximum_fusion.gain_ref), custom_call_target="tpu_custom_call" | custom-call | flops 209715200 | bytes 8388608 | tf_op jit(solution)/shard_map/prep/pallas_call | solution.py:155
  329.1 9.3 %place.5 = (bf16[8,2560,1024]{2,1,0:T(8,128)(2,1)}, bf16[2,160,8192]{2,1,0:T(8,128)(2,1)}) custom-call(s32[3]{0:T(128)} %pad_add_fusion.3.where_ref, bf16[1280,1024]{1,0:T(8,128)(2,1)} %cut.3.refs_0_, bf16[1280,1024]{1,0:T(8,128)(2,1)} %cut.4.refs_1_, bf16[1280,1024]{1,0:T(8,128)(2,1)} %collective-permute-done.12.refs_2_, ...), custom_call_target="tpu_custom_call" | custom-call | flops 1048576000 | bytes 20971520 | tf_op jit(solution)/shard_map/place/pallas_call | solution.py:127
  338.4 4.3 collective-permute-start.25
  342.7 9.3 %place.6 = (bf16[8,2560,1024]{2,1,0:T(8,128)(2,1)}, bf16[2,160,8192]{2,1,0:T(8,128)(2,1)}) custom-call(s32[5]{0:T(128)} %pad_add_fusion.2.where_ref, bf16[1280,1024]{1,0:T(8,128)(2,1)} %collective-permute-done.9.refs_0_, bf16[1280,1024]{1,0:T(8,128)(2,1)} %collective-permute-done.10.refs_1_, ...), custom_call_target="tpu_custom_call", output_to_operand_aliasing={{0}: (5, {}), {1}: (6, {})} | custom-call | flops 1048576000 | bytes 20971520 | tf_op jit(solution)/shard_map/place/pallas_call | solution.py:127
  352.2 9.3 %place.7 = (bf16[8,2560,1024]{2,1,0:T(8,128)(2,1)}, bf16[2,160,8192]{2,1,0:T(8,128)(2,1)}) custom-call(s32[5]{0:T(128)} %pad_add_fusion.2.where_ref, bf16[1280,1024]{1,0:T(8,128)(2,1)} %collective-permute-done.3.refs_0_, bf16[1280,1024]{1,0:T(8,128)(2,1)} %collective-permute-done.6.refs_1_, ...), custom_call_target="tpu_custom_call", output_to_operand_aliasing={{0}: (5, {}), {1}: (6, {})} | custom-call | flops 1048576000 | bytes 20971520 | tf_op jit(solution)/shard_map/place/pallas_call | solution.py:127
  361.5 33.2 %early.2.refs_2_ = f32[2560,1024]{1,0:T(8,128)} custom-call(s32[8]{0:T(128)} %pad_add_fusion.4.which_ref, bf16[3,1024,2048]{2,1,0:T(8,128)(2,1)} %prep.15.refs_0_.x_hbm, bf16[4,2,2560,1024]{3,2,1,0:T(8,128)(2,1)} %bitcast.17, bf16[4,2,2560,1024]{3,2,1,0:T(8,128)(2,1)} %bitcast.18), custom_call_target="tpu_custom_call" | custom-call | flops 21474836480 | bytes 39845888 | tf_op jit(solution)/shard_map/early/pallas_call | solution.py:235
  399.6 5.4 %place.8 = (bf16[8,2560,1024]{2,1,0:T(8,128)(2,1)}, bf16[2,160,8192]{2,1,0:T(8,128)(2,1)}) custom-call(s32[2]{0:T(128)} %pad_add_fusion.1.where_ref, bf16[1280,1024]{1,0:T(8,128)(2,1)} %collective-permute-done.1.refs_0_, bf16[1280,1024]{1,0:T(8,128)(2,1)} %collective-permute-done.4.refs_1_, ...), custom_call_target="tpu_custom_call", output_to_operand_aliasing={{0}: (3, {}), {1}: (4, {})} | custom-call | flops 524288000 | bytes 10485760 | tf_op jit(solution)/shard_map/place/pallas_call | solution.py:127
  405.1 5.1 %collective-permute-start.28 = (bf16[256,2048]{1,0:T(8,128)(2,1)}, bf16[256,2048]{1,0:T(8,128)(2,1)}, u32[]{:S(2)}, u32[]{:S(2)}) collective-permute-start(bf16[256,2048]{1,0:T(8,128)(2,1)} %collective-permute-done.24.x_ref), channel_id=1, source_target_pairs={{0,24},{8,0},{16,8},{24,16},{1,25},{9,1},{17,9},{25,17},{2,26},{10... | collective-permute-start | bytes 3145736 | tf_op jit(solution)/shard_map/ppermute | solution.py:465
  410.2 5.4 %place.9 = (bf16[8,2560,1024]{2,1,0:T(8,128)(2,1)}, bf16[2,160,8192]{2,1,0:T(8,128)(2,1)}) custom-call(s32[2]{0:T(128)} %pad_add_fusion.where_ref, bf16[1280,1024]{1,0:T(8,128)(2,1)} %collective-permute-done.2.refs_0_, bf16[1280,1024]{1,0:T(8,128)(2,1)} %collective-permute-done.5.refs_1_, ...), custom_call_target="tpu_custom_call", output_to_operand_aliasing={{0}: (3, {}), {1}: (4, {})} | custom-call | flops 524288000 | bytes 10485760 | tf_op jit(solution)/shard_map/place/pallas_call | solution.py:127
  415.6 23.6 %early.3.refs_2_.refs_4_.refs_6_ = f32[2560,1024]{1,0:T(8,128)} custom-call(s32[8]{0:T(128)} %pad_add_fusion.5.which_ref, bf16[3,1024,2048]{2,1,0:T(8,128)(2,1)} %prep.17.x_hbm, bf16[4,2,2560,1024]{3,2,1,0:T(8,128)(2,1)} %bitcast.19, bf16[4,2,2560,1024]{3,2,1,0:T(8,128)(2,1)} %bitcast.20, f32[2560,1024]{1,0:T(8,128)} %early.2.refs_2_), custom_call_target="tpu_custom_call", output_to_operand_aliasing={{}: (4, {})} | custom-call | flops 21474836480 | bytes 50331648 | tf_op jit(solution)/shard_map/early/pallas_call | solution.py:235
  439.2 13.3 %late.4 = (bf16[1024,2048]{1,0:T(8,128)(2,1)}, bf16[2,256,128]{2,1,0:T(8,128)(2,1)}, bf16[2,128,256]{2,1,0:T(8,128)(2,1)}) custom-call(s32[1]{0:T(128)} %slice.57.which_ref, f32[1024,1]{1,0:T(8,128)} %add_rsqrt_fusion.inv_ref, f32[4,2048]{1,0:T(4,128)} %pad_maximum_fusion.gain_ref, f32[64,1024]{1,0:T(8,128)} %get-tuple-element.46.cos_ref, ...), custom_call_target="tpu_custom_call" | custom-call | flops 3221225472 | bytes 14155776 | tf_op jit(solution)/shard_map/late/pallas_call | solution.py:386
  452.5 14.4 %late.5 = (bf16[1024,2048]{1,0:T(8,128)(2,1)}, bf16[2,256,128]{2,1,0:T(8,128)(2,1)}, bf16[2,128,256]{2,1,0:T(8,128)(2,1)}) custom-call(s32[1]{0:T(128)} %slice.57.which_ref, f32[1024,1]{1,0:T(8,128)} %add_rsqrt_fusion.inv_ref, f32[4,2048]{1,0:T(4,128)} %pad_maximum_fusion.gain_ref, ...), custom_call_target="tpu_custom_call", output_to_operand_aliasing={{0}: (11, {})} | custom-call | flops 3758096384 | bytes 14155776 | tf_op jit(solution)/shard_map/late/pallas_call | solution.py:386
  467.0 14.6 %late.6 = (bf16[1024,2048]{1,0:T(8,128)(2,1)}, bf16[2,256,128]{2,1,0:T(8,128)(2,1)}, bf16[2,128,256]{2,1,0:T(8,128)(2,1)}) custom-call(s32[1]{0:T(128)} %slice.57.which_ref, f32[1024,1]{1,0:T(8,128)} %add_rsqrt_fusion.inv_ref, f32[4,2048]{1,0:T(4,128)} %pad_maximum_fusion.gain_ref, ...), custom_call_target="tpu_custom_call", output_to_operand_aliasing={{0}: (13, {})} | custom-call | flops 4294967296 | bytes 14155776 | tf_op jit(solution)/shard_map/late/pallas_call | solution.py:386
  481.6 14.6 %late.7 = (bf16[1024,2048]{1,0:T(8,128)(2,1)}, bf16[2,256,128]{2,1,0:T(8,128)(2,1)}, bf16[2,128,256]{2,1,0:T(8,128)(2,1)}) custom-call(s32[1]{0:T(128)} %slice.57.which_ref, f32[1024,1]{1,0:T(8,128)} %add_rsqrt_fusion.inv_ref, f32[4,2048]{1,0:T(4,128)} %pad_maximum_fusion.gain_ref, ...), custom_call_target="tpu_custom_call", output_to_operand_aliasing={{0}: (13, {})} | custom-call | flops 4294967296 | bytes 14155776 | tf_op jit(solution)/shard_map/late/pallas_call | solution.py:386
  (105 shorter events, 65.2 us)
Async XLA Ops:
  3.3 158.4 %collective-permute-start.12 = (bf16[1280,1024]{1,0:T(8,128)(2,1)}, bf16[1280,1024]{1,0:T(8,128)(2,1)}, u32[]{:S(2)}, u32[]{:S(2)}) collective-permute-start(bf16[1280,1024]{1,0:T(8,128)(2,1)} %cut.3.refs_0_), channel_id=1, source_target_pairs={{0,1},{1,0},{2,3},{3,2},{4,5},{5,4},{6,7},{7,6},{8,9},{9,8},{10,11... | collective-permute-start | bytes 7864328 | tf_op jit(solution)/shard_map/ppermute | solution.py:472
  3.8 158.4 %collective-permute-start = (bf16[1280,1024]{1,0:T(8,128)(2,1)}, bf16[1280,1024]{1,0:T(8,128)(2,1)}, u32[]{:S(2)}, u32[]{:S(2)}) collective-permute-start(bf16[1280,1024]{1,0:T(8,128)(2,1)} %cut.3.refs_0_), channel_id=1, source_target_pairs={{0,4},{1,5},{2,6},{3,7},{4,0},{5,1},{6,2},{7,3},{8,12},{9,13},{10,... | collective-permute-start | bytes 7864328 | tf_op jit(solution)/shard_map/ppermute | solution.py:472
  8.4 64.6 %collective-permute-start.19 = (bf16[256,2048]{1,0:T(8,128)(2,1)}, bf16[256,2048]{1,0:T(8,128)(2,1)}, u32[]{:S(2)}, u32[]{:S(2)}) collective-permute-start(bf16[256,2048]{1,0:T(8,128)(2,1)} %cut.5), channel_id=1, source_target_pairs={{0,24},{8,0},{16,8},{24,16},{1,25},{9,1},{17,9},{25,17},{2,26},{10... | collective-permute-start | bytes 3145736 | tf_op jit(solution)/shard_map/ppermute | solution.py:465
  15.2 57.9 %collective-permute-start.14 = (bf16[256,2048]{1,0:T(8,128)(2,1)S(1)}, bf16[256,2048]{1,0:T(8,128)(2,1)}, u32[]{:S(2)}, u32[]{:S(2)}) collective-permute-start(bf16[256,2048]{1,0:T(8,128)(2,1)S(1)} %get-tuple-element.64), channel_id=1, source_target_pairs={{0,24},{8,0},{16,8},{24,16},{1,25},{9,1},{17,9},{25,17},{2,26},{10... | collective-permute-start | bytes 3145736 | tf_op jit(solution)/shard_map/ppermute | solution.py:465
  73.0 46.1 %collective-permute-start.21 = (bf16[256,2048]{1,0:T(8,128)(2,1)}, bf16[256,2048]{1,0:T(8,128)(2,1)}, u32[]{:S(2)}, u32[]{:S(2)}) collective-permute-start(bf16[256,2048]{1,0:T(8,128)(2,1)} %get-tuple-element.63), channel_id=1, source_target_pairs={{0,24},{8,0},{16,8},{24,16},{1,25},{9,1},{17,9},{25,17},{2,26},{10... | collective-permute-start | bytes 3145736 | tf_op jit(solution)/shard_map/ppermute | solution.py:465
  73.1 68.5 %collective-permute-start.20 = (bf16[256,2048]{1,0:T(8,128)(2,1)}, bf16[256,2048]{1,0:T(8,128)(2,1)}, u32[]{:S(2)}, u32[]{:S(2)}) collective-permute-start(bf16[256,2048]{1,0:T(8,128)(2,1)} %collective-permute-done.19.x_ref), channel_id=1, source_target_pairs={{0,24},{8,0},{16,8},{24,16},{1,25},{9,1},{17,9},{25,17},{2,26},{10... | collective-permute-start | bytes 3145736 | tf_op jit(solution)/shard_map/ppermute | solution.py:465
  96.6 63.6 %collective-permute-start.15 = (bf16[256,2048]{1,0:T(8,128)(2,1)}, bf16[256,2048]{1,0:T(8,128)(2,1)}, u32[]{:S(2)}, u32[]{:S(2)}) collective-permute-start(bf16[256,2048]{1,0:T(8,128)(2,1)} %collective-permute-done.14.x_ref), channel_id=1, source_target_pairs={{0,24},{8,0},{16,8},{24,16},{1,25},{9,1},{17,9},{25,17},{2,26},{10... | collective-permute-start | bytes 3145736 | tf_op jit(solution)/shard_map/ppermute | solution.py:465
  141.6 60.1 %collective-permute-start.3 = (bf16[1280,1024]{1,0:T(8,128)(2,1)}, bf16[1280,1024]{1,0:T(8,128)(2,1)}, u32[]{:S(2)}, u32[]{:S(2)}) collective-permute-start(bf16[1280,1024]{1,0:T(8,128)(2,1)} %cut.4.refs_1_), channel_id=1, source_target_pairs={{0,2},{1,3},{2,0},{3,1},{4,6},{5,7},{6,4},{7,5},{8,10},{9,11},{10,... | collective-permute-start | bytes 7864328 | tf_op jit(solution)/shard_map/ppermute | solution.py:472
  160.2 97.6 %collective-permute-start.9 = (bf16[1280,1024]{1,0:T(8,128)(2,1)}, bf16[1280,1024]{1,0:T(8,128)(2,1)}, u32[]{:S(2)}, u32[]{:S(2)}) collective-permute-start(bf16[1280,1024]{1,0:T(8,128)(2,1)} %cut.3.refs_0_), channel_id=1, source_target_pairs={{0,2},{1,3},{2,0},{3,1},{4,6},{5,7},{6,4},{7,5},{8,10},{9,11},{10,... | collective-permute-start | bytes 7864328 | tf_op jit(solution)/shard_map/ppermute | solution.py:472
  161.7 96.1 %collective-permute-start.7 = (bf16[1280,1024]{1,0:T(8,128)(2,1)}, bf16[1280,1024]{1,0:T(8,128)(2,1)}, u32[]{:S(2)}, u32[]{:S(2)}) collective-permute-start(bf16[1280,1024]{1,0:T(8,128)(2,1)} %cut.4.refs_1_), channel_id=1, source_target_pairs={{0,4},{1,5},{2,6},{3,7},{4,0},{5,1},{6,2},{7,3},{8,12},{9,13},{10,... | collective-permute-start | bytes 7864328 | tf_op jit(solution)/shard_map/ppermute | solution.py:472
  162.2 96.1 %collective-permute-start.11 = (bf16[1280,1024]{1,0:T(8,128)(2,1)}, bf16[1280,1024]{1,0:T(8,128)(2,1)}, u32[]{:S(2)}, u32[]{:S(2)}) collective-permute-start(bf16[1280,1024]{1,0:T(8,128)(2,1)} %collective-permute-done.refs_2_), channel_id=1, source_target_pairs={{0,1},{1,0},{2,3},{3,2},{4,5},{5,4},{6,7},{7,6},{8,9},{9,8},{10,11... | collective-permute-start | bytes 7864328 | tf_op jit(solution)/shard_map/ppermute | solution.py:472
  162.3 143.2 %collective-permute-start.1 = (bf16[1280,1024]{1,0:T(8,128)(2,1)}, bf16[1280,1024]{1,0:T(8,128)(2,1)}, u32[]{:S(2)}, u32[]{:S(2)}) collective-permute-start(bf16[1280,1024]{1,0:T(8,128)(2,1)} %collective-permute-done.refs_2_), channel_id=1, source_target_pairs={{0,2},{1,3},{2,0},{3,1},{4,6},{5,7},{6,4},{7,5},{8,10},{9,11},{10,... | collective-permute-start | bytes 7864328 | tf_op jit(solution)/shard_map/ppermute | solution.py:472
  201.7 103.8 %collective-permute-start.4 = (bf16[1280,1024]{1,0:T(8,128)(2,1)}, bf16[1280,1024]{1,0:T(8,128)(2,1)}, u32[]{:S(2)}, u32[]{:S(2)}) collective-permute-start(bf16[1280,1024]{1,0:T(8,128)(2,1)} %collective-permute-done.3.refs_0_), channel_id=1, source_target_pairs={{0,4},{1,5},{2,6},{3,7},{4,0},{5,1},{6,2},{7,3},{8,12},{9,13},{10,... | collective-permute-start | bytes 7864328 | tf_op jit(solution)/shard_map/ppermute | solution.py:472
  257.9 94.2 %collective-permute-start.6 = (bf16[1280,1024]{1,0:T(8,128)(2,1)}, bf16[1280,1024]{1,0:T(8,128)(2,1)}, u32[]{:S(2)}, u32[]{:S(2)}) collective-permute-start(bf16[1280,1024]{1,0:T(8,128)(2,1)} %collective-permute-done.3.refs_0_), channel_id=1, source_target_pairs={{0,1},{1,0},{2,3},{3,2},{4,5},{5,4},{6,7},{7,6},{8,9},{9,8},{10,11... | collective-permute-start | bytes 7864328 | tf_op jit(solution)/shard_map/ppermute | solution.py:472
  257.9 80.5 %collective-permute-start.10 = (bf16[1280,1024]{1,0:T(8,128)(2,1)}, bf16[1280,1024]{1,0:T(8,128)(2,1)}, u32[]{:S(2)}, u32[]{:S(2)}) collective-permute-start(bf16[1280,1024]{1,0:T(8,128)(2,1)} %collective-permute-done.9.refs_0_), channel_id=1, source_target_pairs={{0,1},{1,0},{2,3},{3,2},{4,5},{5,4},{6,7},{7,6},{8,9},{9,8},{10,11... | collective-permute-start | bytes 7864328 | tf_op jit(solution)/shard_map/ppermute | solution.py:472
  258.4 93.7 %collective-permute-start.8 = (bf16[1280,1024]{1,0:T(8,128)(2,1)}, bf16[1280,1024]{1,0:T(8,128)(2,1)}, u32[]{:S(2)}, u32[]{:S(2)}) collective-permute-start(bf16[1280,1024]{1,0:T(8,128)(2,1)} %collective-permute-done.7.refs_2_), channel_id=1, source_target_pairs={{0,1},{1,0},{2,3},{3,2},{4,5},{5,4},{6,7},{7,6},{8,9},{9,8},{10,11... | collective-permute-start | bytes 7864328 | tf_op jit(solution)/shard_map/ppermute | solution.py:472
  305.4 99.6 %collective-permute-start.2 = (bf16[1280,1024]{1,0:T(8,128)(2,1)}, bf16[1280,1024]{1,0:T(8,128)(2,1)}, u32[]{:S(2)}, u32[]{:S(2)}) collective-permute-start(bf16[1280,1024]{1,0:T(8,128)(2,1)} %collective-permute-done.1.refs_0_), channel_id=1, source_target_pairs={{0,1},{1,0},{2,3},{3,2},{4,5},{5,4},{6,7},{7,6},{8,9},{9,8},{10,11... | collective-permute-start | bytes 7864328 | tf_op jit(solution)/shard_map/ppermute | solution.py:472
  305.4 104.7 %collective-permute-start.5 = (bf16[1280,1024]{1,0:T(8,128)(2,1)}, bf16[1280,1024]{1,0:T(8,128)(2,1)}, u32[]{:S(2)}, u32[]{:S(2)}) collective-permute-start(bf16[1280,1024]{1,0:T(8,128)(2,1)} %collective-permute-done.4.refs_1_), channel_id=1, source_target_pairs={{0,1},{1,0},{2,3},{3,2},{4,5},{5,4},{6,7},{7,6},{8,9},{9,8},{10,11... | collective-permute-start | bytes 7864328 | tf_op jit(solution)/shard_map/ppermute | solution.py:472
  338.4 56.3 %collective-permute-start.25 = (bf16[256,2048]{1,0:T(8,128)(2,1)}, bf16[256,2048]{1,0:T(8,128)(2,1)}, u32[]{:S(2)}, u32[]{:S(2)}) collective-permute-start(bf16[256,2048]{1,0:T(8,128)(2,1)} %collective-permute-done.22.x_ref), channel_id=1, source_target_pairs={{0,24},{8,0},{16,8},{24,16},{1,25},{9,1},{17,9},{25,17},{2,26},{10... | collective-permute-start | bytes 3145736 | tf_op jit(solution)/shard_map/ppermute | solution.py:465
  352.0 45.2 %collective-permute-start.24 = (bf16[256,2048]{1,0:T(8,128)(2,1)}, bf16[256,2048]{1,0:T(8,128)(2,1)}, u32[]{:S(2)}, u32[]{:S(2)}) collective-permute-start(bf16[256,2048]{1,0:T(8,128)(2,1)} %collective-permute-done.21.x_ref), channel_id=1, source_target_pairs={{0,24},{8,0},{16,8},{24,16},{1,25},{9,1},{17,9},{25,17},{2,26},{10... | collective-permute-start | bytes 3145736 | tf_op jit(solution)/shard_map/ppermute | solution.py:465
  352.1 87.1 %collective-permute-start.23 = (bf16[256,2048]{1,0:T(8,128)(2,1)}, bf16[256,2048]{1,0:T(8,128)(2,1)}, u32[]{:S(2)}, u32[]{:S(2)}) collective-permute-start(bf16[256,2048]{1,0:T(8,128)(2,1)} %collective-permute-done.20.x_ref), channel_id=1, source_target_pairs={{0,24},{8,0},{16,8},{24,16},{1,25},{9,1},{17,9},{25,17},{2,26},{10... | collective-permute-start | bytes 3145736 | tf_op jit(solution)/shard_map/ppermute | solution.py:465
  394.7 57.8 %collective-permute-start.26 = (bf16[256,2048]{1,0:T(8,128)(2,1)}, bf16[256,2048]{1,0:T(8,128)(2,1)}, u32[]{:S(2)}, u32[]{:S(2)}) collective-permute-start(bf16[256,2048]{1,0:T(8,128)(2,1)} %collective-permute-done.15.x_ref), channel_id=1, source_target_pairs={{0,24},{8,0},{16,8},{24,16},{1,25},{9,1},{17,9},{25,17},{2,26},{10... | collective-permute-start | bytes 3145736 | tf_op jit(solution)/shard_map/ppermute | solution.py:465
  397.2 69.8 %collective-permute-start.27 = (bf16[256,2048]{1,0:T(8,128)(2,1)}, bf16[256,2048]{1,0:T(8,128)(2,1)}, u32[]{:S(2)}, u32[]{:S(2)}) collective-permute-start(bf16[256,2048]{1,0:T(8,128)(2,1)} %collective-permute-done.25.x_ref), channel_id=1, source_target_pairs={{0,24},{8,0},{16,8},{24,16},{1,25},{9,1},{17,9},{25,17},{2,26},{10... | collective-permute-start | bytes 3145736 | tf_op jit(solution)/shard_map/ppermute | solution.py:465
  405.1 76.6 %collective-permute-start.28 = (bf16[256,2048]{1,0:T(8,128)(2,1)}, bf16[256,2048]{1,0:T(8,128)(2,1)}, u32[]{:S(2)}, u32[]{:S(2)}) collective-permute-start(bf16[256,2048]{1,0:T(8,128)(2,1)} %collective-permute-done.24.x_ref), channel_id=1, source_target_pairs={{0,24},{8,0},{16,8},{24,16},{1,25},{9,1},{17,9},{25,17},{2,26},{10... | collective-permute-start | bytes 3145736 | tf_op jit(solution)/shard_map/ppermute | solution.py:465
  (10 other events, 515.8 us)
